TPU v7x, 256 devices: a whole 4x4x8 slice. The times are simulated.
256 devices in a mesh: dp: 64 (over z, y, core), comp: 4 (over x).
Axes of the slice: x: 4, y: 4, z: 8, core: 2. Of those that a mesh axis runs over, the one named last changes fastest.
Arguments:
- points: float32 [65536, 128], P('dp'), may hold values from -64 to 64
- block_counts: int32 [64], replicated, may hold values from 1 to 16, as said below
- block_dest: int32 [64, 16], replicated, may hold values from 0 to 63, as said below
- means: float32 [256, 128], P(('dp', 'comp')), may hold values from -3 to 3
- factors: float32 [256, 128, 128], P(('dp', 'comp')), may hold values from -0.25 to 1.4, as said below
- log_weights: float32 [256], P(('dp', 'comp')), may hold values from -4 to 4
Outputs:
- new_means: float32 [256, 128], P(('dp', 'comp'))
- new_factors: float32 [256, 128, 128], P(('dp', 'comp'))
- new_log_weights: float32 [256], P(('dp', 'comp'))
- log_density: float32 [16384], P('dp')
Inputs may be any that keep to these rules, and one draw needn't show every extreme that they name: `block_counts`: blocks live on each index of dp on entry; they sum to 256, and one index holds exactly 16. `block_dest`: for j < block_counts[s], the index of dp that receives block j of index s; every index receives exactly 4 blocks, no index sends more than 1 block to one index, and some index sends exactly 1 to one; entries with j >= block_counts[s] are unused. `factors`: each matrix is upper triangular with diagonal entries from 0.7 to 1.4.
All inputs are finite; a program needn't handle non-finite values.
Results may differ from a plain program's by a relative error of at most 0.003.
Values sent between devices are 32-bit elements; how exact they have to be, the bound alone decides.
A program may use at most 128 MiB of HBM per device.

v0:
```python
import math

import jax
import jax.numpy as jnp
from jax import lax
from jax.sharding import Mesh
from jax.sharding import PartitionSpec as P

K = 256
RB = 4
ITERS = 2
DP = ("dp_0", "dp_1", "dp_2")
DP_COMP = ("dp_0", "dp_1", "dp_2", "comp")


highest = lax.Precision.HIGHEST
ridge_term = 1.0
log_two_pi = math.log(2.0 * math.pi)


def laid_out(pieces, dim):
    pieces = jnp.moveaxis(pieces, 0, dim)
    dims = pieces.shape
    return pieces.reshape(*dims[:dim], dims[dim] * dims[dim + 1], *dims[dim + 2 :])


def stacked_from(value, axes, sequence):
    pieces = value[None]
    for k in sequence:
        pieces = lax.all_gather(pieces, axes[k], axis=0, tiled=True)
    block = [lax.axis_size(axes[k]) for k in reversed(sequence)]
    pieces = pieces.reshape(*block, *value.shape)
    turned = sorted(range(len(sequence)), key=lambda place: sequence[len(sequence) - 1 - place])
    return pieces.transpose(*turned, *range(len(sequence), pieces.ndim)).reshape(-1, *value.shape)


def gathered_by_axis(value, axes, sequence, dim):
    return laid_out(stacked_from(value, axes, sequence), dim)


def copy_for_each(value, axis):
    copies = jnp.broadcast_to(value, (lax.axis_size(axis), *value.shape))
    return lax.all_to_all(copies, axis, split_axis=0, concat_axis=0, tiled=True)


def gathered_once(value, axis):
    leaves = jax.tree.leaves(value)
    sequence = sorted(range(len(leaves)), key=lambda k: -leaves[k].size)
    width = (1, *leaves[sequence[0]].shape)[-1]
    lines = [
        jnp.pad(leaves[k].reshape(-1), (0, -leaves[k].size % width)).reshape(-1, width)
        for k in sequence
    ]
    both, at, found = (copy_for_each(jnp.concatenate(lines), axis), 0, {})
    for k, line in zip(sequence, lines):
        piece = both[:, at : at + len(line)].reshape(len(both), -1)
        found[k] = piece[:, : leaves[k].size].reshape(-1, *leaves[k].shape)
        at += len(line)
    numbers = iter(range(len(leaves)))
    return jax.tree.map(lambda _: found[next(numbers)], value)


def combined_pairwise(pieces, combine):
    while len(jax.tree.leaves(pieces)[0]) > 1:
        pieces = jax.vmap(combine)(
            *(jax.tree.map(lambda part: part[side::2], pieces) for side in (0, 1))
        )
    return jax.tree.map(lambda part: part[0], pieces)


def merged(value, axis, combine):
    pieces = gathered_once(value, axis)
    return combined_pairwise(pieces, combine)


def in_blocks(value, dim, size):
    before, after = (value.shape[:dim], value.shape[dim + 1 :])
    return jnp.moveaxis(value.reshape(*before, size, -1, *after), dim, 0)


def summed_on_arrival(value, axis, dim):
    size = lax.axis_size(axis)
    pieces = lax.all_to_all(in_blocks(value, dim, size), axis, 0, 0, tiled=True)
    return jnp.sum(pieces, axis=0)


def rebalance_rows(points, block_counts, block_dest):
    dp_devices = lax.axis_size(DP)
    dp_index = lax.axis_index(DP)
    nblocks = block_dest.shape[1]
    feature_width = points.shape[1]
    block_rows = points.shape[0] // nblocks
    slot_count = (nblocks + dp_devices - 1) // dp_devices
    blocks = points.reshape(nblocks, block_rows, feature_width)
    my_dest = lax.dynamic_index_in_dim(block_dest, dp_index, 0, keepdims=False)
    my_count = lax.dynamic_index_in_dim(block_counts, dp_index, 0, keepdims=False)
    positions = jnp.arange(nblocks, dtype=jnp.int32)
    targets = jnp.arange(dp_devices, dtype=jnp.int32)
    slot_ids = jnp.arange(slot_count, dtype=jnp.int32)
    send_hits = ((my_dest[:, None] == targets[None, :]) & (positions[:, None] < my_count)).astype(
        jnp.int32
    )
    send_rank = jnp.cumsum(send_hits, axis=0) - send_hits
    chosen = send_hits[:, :, None] * (send_rank[:, :, None] == slot_ids[None, None, :]).astype(
        jnp.int32
    )
    filled = jnp.sum(chosen, axis=0)
    source_block = jnp.sum(chosen * positions[:, None, None], axis=0)
    picked = jnp.take(blocks, source_block.reshape(-1), axis=0).reshape(
        dp_devices, slot_count, block_rows, feature_width
    )
    outgoing = jnp.where(filled[:, :, None, None] > 0, picked, 0.0)
    incoming = lax.all_to_all(outgoing, DP, split_axis=0, concat_axis=0, tiled=True)
    live_all = positions[None, :] < block_counts[:, None]
    sent_here = jnp.sum(((block_dest == dp_index) & live_all).astype(jnp.int32), axis=1)
    full_slot = (slot_ids[None, :] < sent_here[:, None]).astype(jnp.int32).reshape(-1)
    order_rank = jnp.cumsum(full_slot) - full_slot
    pick_slots = jnp.arange(RB, dtype=jnp.int32)
    pick_table = full_slot[None, :] * (order_rank[None, :] == pick_slots[:, None]).astype(jnp.int32)
    pick_index = jnp.sum(
        pick_table * jnp.arange(dp_devices * slot_count, dtype=jnp.int32)[None, :], axis=1
    )
    arrived = jnp.take(
        incoming.reshape(dp_devices * slot_count, block_rows, feature_width), pick_index, axis=0
    )
    return arrived.reshape(RB * block_rows, feature_width)


def densities(points_live, centres, factor_set, weights):
    members = centres.shape[0]
    group_width = math.gcd(members, 8)
    feature_width = centres.shape[1]

    def block_density(inputs):
        centre_set, factor_block, weight_block = inputs
        shifted = points_live[None, :, :] - centre_set[:, None, :]
        projected = jnp.einsum("grd,gde->gre", shifted, factor_block, precision=highest)
        logdet = jnp.sum(jnp.log(jnp.diagonal(factor_block, axis1=1, axis2=2)), axis=1)
        offset_terms = weight_block + logdet - 0.5 * feature_width * log_two_pi
        return offset_terms[:, None] - 0.5 * jnp.sum(projected * projected, axis=2)

    grouped = lax.map(
        block_density,
        (
            centres.reshape(members // group_width, group_width, feature_width),
            factor_set.reshape(members // group_width, group_width, feature_width, feature_width),
            weights.reshape(members // group_width, group_width),
        ),
    )
    return grouped.reshape(members, points_live.shape[0])


def moments(points_live, centres, responsibility):
    members = centres.shape[0]
    group_width = math.gcd(members, 8)
    feature_width = centres.shape[1]

    def block_moments(inputs):
        centre_set, weight_block = inputs
        shifted = points_live[None, :, :] - centre_set[:, None, :]
        weight_sum = jnp.sum(weight_block, axis=1)
        first_moment = jnp.einsum("gr,grd->gd", weight_block, shifted, precision=highest)
        second_moment = jnp.einsum(
            "grd,gre->gde", shifted * weight_block[:, :, None], shifted, precision=highest
        )
        return (weight_sum, first_moment, second_moment)

    weight_sums, firsts, seconds = lax.map(
        block_moments,
        (
            centres.reshape(members // group_width, group_width, feature_width),
            responsibility.reshape(members // group_width, group_width, responsibility.shape[1]),
        ),
    )
    return (
        weight_sums.reshape(members),
        firsts.reshape(members, feature_width),
        seconds.reshape(members, feature_width, feature_width),
    )


def pack_symmetric(matrix):
    half_width = matrix.shape[-1] // 2
    top_left = jnp.triu(matrix[:, :half_width, :half_width]) + jnp.tril(
        matrix[:, half_width:, half_width:], -1
    )
    packed = jnp.concatenate([top_left, matrix[:, :half_width, half_width:]], axis=2)
    corner = jnp.diagonal(matrix[:, half_width:, half_width:], axis1=1, axis2=2)
    return (packed, corner)


def unpack_symmetric(packed, corner):
    half_width = packed.shape[1]
    identity = jnp.eye(half_width, dtype=jnp.float32)
    top_left = packed[:, :, :half_width]
    right_block = packed[:, :, half_width:]
    first_block = jnp.triu(top_left) + jnp.swapaxes(jnp.triu(top_left, 1), 1, 2)
    strict_part = jnp.tril(top_left, -1)
    last_block = strict_part + jnp.swapaxes(strict_part, 1, 2) + corner[:, :, None] * identity
    upper_rows = jnp.concatenate([first_block, right_block], axis=2)
    lower_rows = jnp.concatenate([jnp.swapaxes(right_block, 1, 2), last_block], axis=2)
    return jnp.concatenate([upper_rows, lower_rows], axis=1)


def pack_upper(matrix):
    half_width = matrix.shape[-1] // 2
    top_left = matrix[:, :half_width, :half_width] + jnp.swapaxes(
        jnp.triu(matrix[:, half_width:, half_width:], 1), 1, 2
    )
    packed = jnp.concatenate([top_left, matrix[:, :half_width, half_width:]], axis=2)
    corner = jnp.diagonal(matrix[:, half_width:, half_width:], axis1=1, axis2=2)
    return (packed, corner)


def unpack_upper(packed, corner):
    half_width = packed.shape[1]
    identity = jnp.eye(half_width, dtype=jnp.float32)
    top_left = packed[:, :, :half_width]
    last_block = jnp.swapaxes(jnp.tril(top_left, -1), 1, 2) + corner[:, :, None] * identity
    upper_rows = jnp.concatenate([jnp.triu(top_left), packed[:, :, half_width:]], axis=2)
    lower_rows = jnp.concatenate([jnp.zeros_like(last_block), last_block], axis=2)
    return jnp.concatenate([upper_rows, lower_rows], axis=1)


def gathered_density(points_live, own_params):
    own_centres, own_factors, own_weights = own_params
    members = own_centres.shape[0] * lax.axis_size(DP)
    feature_width = own_centres.shape[1]
    initial = (
        jnp.zeros((members, points_live.shape[0]), jnp.float32),
        jnp.zeros((members, feature_width), jnp.float32),
    )
    packed, corner = pack_upper(own_factors)
    centre_piece = gathered_by_axis(own_centres, DP, (1, 0, 2), 0)
    offset = jnp.int32(0)
    log_table = lax.dynamic_update_slice_in_dim(
        initial[0],
        densities(
            points_live,
            centre_piece,
            unpack_upper(
                gathered_by_axis(packed, DP, (1, 0, 2), 0),
                gathered_by_axis(corner, DP, (1, 0, 2), 0),
            ),
            gathered_by_axis(own_weights, DP, (1, 0, 2), 0),
        ),
        offset,
        0,
    )
    centres = lax.dynamic_update_slice_in_dim(initial[1], centre_piece, offset, 0)
    return (log_table, centres)


def row_responsibility(log_table):
    row_peak = jnp.max(log_table, axis=0)
    row_scaled = jnp.sum(jnp.exp(log_table - row_peak[None, :]), axis=0)

    def combine(earlier, later):
        joint_peak = jnp.maximum(earlier[0], later[0])
        return (
            joint_peak,
            earlier[1] * jnp.exp(earlier[0] - joint_peak)
            + later[1] * jnp.exp(later[0] - joint_peak),
        )

    peak_all, scaled_all = merged((row_peak, row_scaled), "comp", combine)
    log_total = peak_all + jnp.log(scaled_all)
    return (log_total, jnp.exp(log_table - log_total[None, :]))


def summed_moments(statistics):
    weight_sum, first_moment, second_moment = statistics
    packed, corner = pack_symmetric(second_moment)
    totals = (
        summed_on_arrival(weight_sum, DP, 0),
        summed_on_arrival(first_moment, DP, 0),
        summed_on_arrival(packed, DP, 0),
        summed_on_arrival(corner, DP, 0),
    )
    return (totals[0], totals[1], unpack_symmetric(totals[2], totals[3]))


def refresh(centres, weight_sum, first_moment, second_moment, total_points):
    identity = jnp.eye(centres.shape[1], dtype=jnp.float32)
    counted = weight_sum + 1.0
    covariance = (
        second_moment
        - first_moment[:, :, None] * first_moment[:, None, :] / counted[:, None, None]
        + ridge_term * identity
    ) / counted[:, None, None]
    cholesky_lower = jnp.linalg.cholesky(covariance)
    inverse_lower = jax.scipy.linalg.solve_triangular(
        cholesky_lower, jnp.broadcast_to(identity, covariance.shape), lower=True
    )
    return (
        centres + first_moment / counted[:, None],
        jnp.swapaxes(inverse_lower, 1, 2),
        jnp.log(counted / total_points),
    )


def per_device(points, block_counts, block_dest, means, factors, log_weights):
    points_live = rebalance_rows(points, block_counts, block_dest)
    total_points = float(lax.axis_size(DP) * points_live.shape[0] + K)
    current = (means, factors, log_weights)
    for iteration in range(ITERS):
        log_table, centres = gathered_density(points_live, current)
        log_total, responsibility = row_responsibility(log_table)
        weight_sum, first_moment, second_moment = summed_moments(
            moments(points_live, centres, responsibility)
        )
        current = refresh(current[0], weight_sum, first_moment, second_moment, total_points)
    new_means, new_factors, new_weights = current
    return (new_means, new_factors, new_weights, log_total / points.shape[1])


def solution(mesh):
    split = Mesh(
        mesh.devices.reshape(8, 4, 2, mesh.shape["comp"]), ("dp_0", "dp_1", "dp_2", "comp")
    )
    in_specs = (P(DP, None), P(), P(), P(DP_COMP, None), P(DP_COMP, None, None), P(DP_COMP))
    out_specs = (P(DP_COMP, None), P(DP_COMP, None, None), P(DP_COMP), P(DP))
    return jax.shard_map(
        per_device, mesh=split, in_specs=in_specs, out_specs=out_specs, check_vma=False
    )
```

profile of v0, /device:TPU:1, one launch (start us, length us, event | category | flops | bytes accessed | tf_op | source)
XLA Modules:
  0.0 927.3 jit_solution(11059183866429565092)
XLA Ops:
  9.2 11.2 %all-gather.3 = f32[4,64,128]{2,1,0:T(8,128)} all-gather(f32[1,64,128]{2,1,0:T(8,128)S(1)} %copy.268), channel_id=5, replica_groups=mesh['dp_0'=8,'dp_1'=4,'dp_2'=2,'comp'=4] {'dp_1'}, dimensions={0}, use_global_device_ids=true | all-gather | bytes 163840 | tf_op jit(solution)/shard_map/all_gather | solution.py:30
  25.8 14.8 %all-to-all-start = ((f32[64,1,64,128]{3,2,1,0:T(8,128)}), f32[64,1,64,128]{3,2,1,0:T(8,128)}, u32[]{:S(2)}, u32[]{:S(2)}) async-start(f32[64,1,64,128]{3,2,1,0:T(8,128)} %fusion.48), calls=%async_computation | async-start | bytes 4194304 | tf_op jit(solution)/shard_map/all_to_all | solution.py:113
  40.7 32.3 %all-gather.26.cloned.1.call-done = f32[32,64,128]{2,1,0:T(8,128)} async-done(((f32[4,64,128]{2,1,0:T(8,128)}), f32[32,64,128]{2,1,0:T(8,128)}) %all-gather.26.cloned.1.call-update) | async-done | bytes 1048592 | tf_op jit(solution)/shard_map/all_gather | solution.py:30
  76.8 8.9 all-reduce.11
  86.2 22.7 %all_gather.79 = f32[32,1,64]{2,1,0:T(1,128)S(1)} all-gather(f32[4,1,64]{2,1,0:T(1,128)S(1)} %reshape.913), channel_id=1, replica_groups=mesh['dp_0'=8,'dp_1'=4,'dp_2'=2,'comp'=4] {'dp_0'}, dimensions={0}, use_global_device_ids=true | all-gather | bytes 9216 | tf_op jit(solution)/shard_map/all_gather | solution.py:30
  118.5 11.6 %all-reduce.3 = f32[32]{0:T(128)S(1)} all-reduce(f32[32]{0:T(128)S(1)} %dynamic-update-slice.3), channel_id=3, replica_groups=mesh['dp_0'=8,'dp_1'=4,'dp_2'=2,'comp'=4] {'dp_0'}, use_global_device_ids=true, to_apply=%add.3 | all-reduce | flops 32 | bytes 256
  144.1 16.2 %all-gather.18 = f32[8,4,128]{2,1,0:T(4,128)S(1)} all-gather(f32[1,4,128]{2,1,0:T(4,128)S(1)} %bitcast.330), channel_id=10, replica_groups=mesh['dp_0'=8,'dp_1'=4,'dp_2'=2,'comp'=4] {'dp_0'}, dimensions={0}, use_global_device_ids=true | all-gather | bytes 18432 | tf_op jit(solution)/shard_map/all_gather | solution.py:30
  160.2 9.8 %all-gather.9 = f32[64,128]{1,0:T(8,128)S(1)} all-gather(f32[32,128]{1,0:T(8,128)S(1)} %bitcast.311), channel_id=11, replica_groups=mesh['dp_0'=8,'dp_1'=4,'dp_2'=2,'comp'=4] {'dp_2'}, dimensions={0}, use_global_device_ids=true | all-gather | bytes 49152 | tf_op jit(solution)/shard_map/all_gather | solution.py:30
  199.3 92.3 %while.52 = (s32[]{:T(128)}, f32[8,8,256]{2,1,0:T(8,128)S(1)}, f32[8,8]{1,0:T(8,128)S(1)}, f32[8,8,128,128]{2,3,1,0:T(8,128)}, f32[4,64,128]{2,1,0:T(8,128)S(1)}, /*index=5*/f32[8,8,128]{2,1,0:T(8,128)S(1)}, s32[]{:T(128)}) while((s32[]{:T(128)}, f32[8,8,256]{2,1,0:T(8,128)S(1)}, f32[8,8]{1,0:T(8,128)S(1)}, f32[8,8,128,128]{2,3,1,0:T(8,128)}, ...), condition=%wide.region_9.10_spmd, body=%wide.region_6.9_spmd.sunk | while | flops 403443200 | bytes 2803933 | solution.py:142
  303.9 31.7 %while.53 = (s32[]{:T(128)}, f32[8,8]{1,0:T(8,128)S(1)}, f32[8,8,128]{2,1,0:T(8,128)}, f32[8,8,128,128]{3,2,1,0:T(8,128)}, f32[8,8,256]{2,1,0:T(8,128)S(1)}, /*i...) while((s32[]{:T(128)}, f32[8,8]{1,0:T(8,128)S(1)}, ...), condition=%wide.region_14.15_spmd, body=%wide.region_12.14_spmd.sunk | while | flops 406849536 | bytes 1254601 | solution.py:168
  355.3 10.3 %all-to-all-start.5 = ((f32[64,1,64]{2,1,0:T(1,128)}), f32[64,1,64]{2,1,0:T(1,128)S(1)}, u32[]{:S(2)}, u32[]{:S(2)}) async-start(f32[64,1,64]{2,1,0:T(1,128)} %copy.297), calls=%async_computation.5 | async-start | bytes 65536 | tf_op jit(solution)/shard_map/all_to_all | solution.py:83
  375.0 8.6 all-to-all-start.2
  392.9 9.1 all-to-all-start.4
  403.9 47.8 %all-to-all-done.4 = f32[64,1,64,128]{3,2,1,0:T(8,128)S(1)} async-done(((f32[64,1,64,128]{3,2,1,0:T(8,128)}), f32[64,1,64,128]{3,2,1,0:T(8,128)S(1)}, u32[]{:S(2)}, u32[]{:S(2)}) %all-to-all-start.4) | async-done | bytes 2097184 | tf_op jit(solution)/shard_map/all_to_all | solution.py:83
  452.5 11.7 %custom-call.20 = f32[1,128,128]{2,1,0:T(8,128)S(1)} custom-call(f32[1,128,128]{2,1,0:T(8,128)S(1)} %fusion.54), custom_call_target="Cholesky" | custom-call | tf_op jit(solution)/shard_map/jit(cholesky)/cholesky | solution.py:291
  465.5 9.8 %custom-call.21 = f32[1,128,128]{1,2,0:T(8,128)S(1)} custom-call(f32[1,128,128]{2,1,0:T(8,128)S(1)} %select_select_fusion.1), custom_call_target="InvertDiagBlocksLowerTriangular" | custom-call | tf_op jit(solution)/shard_map/jit(_solve_triangular)/triangular_solve | solution.py:292
  475.9 10.2 %all-gather.10 = f32[4,64,128]{2,1,0:T(8,128)} all-gather(f32[1,64,128]{2,1,0:T(8,128)S(1)} %copy.302), channel_id=12, replica_groups=mesh['dp_0'=8,'dp_1'=4,'dp_2'=2,'comp'=4] {'dp_1'}, dimensions={0}, use_global_device_ids=true | all-gather | bytes 163840 | tf_op jit(solution)/shard_map/all_gather | solution.py:30
  486.2 31.5 %all-gather.30.cloned.1.call-done = f32[32,64,128]{2,1,0:T(8,128)} async-done(((f32[4,64,128]{2,1,0:T(8,128)}), f32[32,64,128]{2,1,0:T(8,128)}) %all-gather.30.cloned.1.call-update) | async-done | bytes 1048592 | tf_op jit(solution)/shard_map/all_gather | solution.py:30
  526.2 16.1 %all-gather.20 = f32[8,4,128]{2,1,0:T(4,128)S(1)} all-gather(f32[1,4,128]{2,1,0:T(4,128)S(1)} %bitcast.331), channel_id=17, replica_groups=mesh['dp_0'=8,'dp_1'=4,'dp_2'=2,'comp'=4] {'dp_0'}, dimensions={0}, use_global_device_ids=true | all-gather | bytes 18432 | tf_op jit(solution)/shard_map/all_gather | solution.py:30
  542.3 14.3 %all-gather.16 = f32[64,128]{1,0:T(8,128)S(1)} all-gather(f32[32,128]{1,0:T(8,128)S(1)} %bitcast.312), channel_id=18, replica_groups=mesh['dp_0'=8,'dp_1'=4,'dp_2'=2,'comp'=4] {'dp_2'}, dimensions={0}, use_global_device_ids=true | all-gather | bytes 49152 | tf_op jit(solution)/shard_map/all_gather | solution.py:30
  563.9 15.7 %all_gather.91 = f32[32,1,64]{2,1,0:T(1,128)S(1)} all-gather(f32[4,1,64]{2,1,0:T(1,128)S(1)} %reshape.920), channel_id=1, replica_groups=mesh['dp_0'=8,'dp_1'=4,'dp_2'=2,'comp'=4] {'dp_0'}, dimensions={0}, use_global_device_ids=true | all-gather | bytes 9216 | tf_op jit(solution)/shard_map/all_gather | solution.py:30
  579.6 9.2 all_gather.92
  589.2 11.6 %all-reduce.7 = f32[32]{0:T(128)S(1)} all-reduce(f32[32]{0:T(128)S(1)} %dynamic-update-slice.7), channel_id=1, replica_groups=mesh['dp_0'=8,'dp_1'=4,'dp_2'=2,'comp'=4] {'dp_0'}, use_global_device_ids=true, to_apply=%add.7 | all-reduce | flops 32 | bytes 256
  639.6 92.3 %while.54 = (s32[]{:T(128)}, f32[8,8,256]{2,1,0:T(8,128)S(1)}, f32[8,8]{1,0:T(8,128)S(1)}, f32[8,8,128,128]{2,3,1,0:T(8,128)}, f32[4,64,128]{2,1,0:T(8,128)S(1)}, /*index=5*/f32[8,8,128]{2,1,0:T(8,128)S(1)}, s32[]{:T(128)}) while((s32[]{:T(128)}, f32[8,8,256]{2,1,0:T(8,128)S(1)}, f32[8,8]{1,0:T(8,128)S(1)}, f32[8,8,128,128]{2,3,1,0:T(8,128)}, ...), condition=%wide.region_24.27_spmd, body=%wide.region_21.26_spmd.sunk | while | flops 403443200 | bytes 2803933 | solution.py:142
  744.7 31.7 %while.55 = (s32[]{:T(128)}, f32[8,8]{1,0:T(8,128)S(1)}, f32[8,8,128]{2,1,0:T(8,128)}, f32[8,8,128,128]{3,2,1,0:T(8,128)}, f32[8,8,256]{2,1,0:T(8,128)S(1)}, /*i...) while((s32[]{:T(128)}, f32[8,8]{1,0:T(8,128)S(1)}, ...), condition=%wide.region_29.32_spmd, body=%wide.region_27.31_spmd.sunk | while | flops 406849536 | bytes 1254601 | solution.py:168
  777.1 8.6 all-to-all-start.8
  798.0 10.3 %all-to-all-start.10 = ((f32[64,1,64]{2,1,0:T(1,128)}), f32[64,1,64]{2,1,0:T(1,128)S(1)}, u32[]{:S(2)}, u32[]{:S(2)}) async-start(f32[64,1,64]{2,1,0:T(1,128)} %copy.327), calls=%async_computation.10 | async-start | bytes 65536 | tf_op jit(solution)/shard_map/all_to_all | solution.py:83
  817.7 8.6 all-to-all-start.7
  835.7 9.5 %all-to-all-start.9 = ((f32[64,1,64,128]{3,2,1,0:T(8,128)}), f32[64,1,64,128]{3,2,1,0:T(8,128)S(1)}, u32[]{:S(2)}, u32[]{:S(2)}) async-start(f32[64,1,64,128]{3,2,1,0:T(8,128)} %copy.321), calls=%async_computation.9 | async-start | bytes 4194304 | tf_op jit(solution)/shard_map/all_to_all | solution.py:83
  847.2 47.5 %all-to-all-done.9 = f32[64,1,64,128]{3,2,1,0:T(8,128)S(1)} async-done(((f32[64,1,64,128]{3,2,1,0:T(8,128)}), f32[64,1,64,128]{3,2,1,0:T(8,128)S(1)}, u32[]{:S(2)}, u32[]{:S(2)}) %all-to-all-start.9) | async-done | bytes 2097184 | tf_op jit(solution)/shard_map/all_to_all | solution.py:83
  895.5 11.7 %custom-call.22 = f32[1,128,128]{2,1,0:T(8,128)S(1)} custom-call(f32[1,128,128]{2,1,0:T(8,128)S(1)} %fusion.52), custom_call_target="Cholesky" | custom-call | tf_op jit(solution)/shard_map/jit(cholesky)/cholesky | solution.py:291
  908.5 9.8 %custom-call.23 = f32[1,128,128]{1,2,0:T(8,128)S(1)} custom-call(f32[1,128,128]{2,1,0:T(8,128)S(1)} %select_select_fusion), custom_call_target="InvertDiagBlocksLowerTriangular" | custom-call | tf_op jit(solution)/shard_map/jit(_solve_triangular)/triangular_solve | solution.py:292
  (492 shorter events, 467.1 us)
Async XLA Ops:
  7.2 16.3 %copy-start = (f32[1024,128]{1,0:T(8,128)S(1)}, f32[1024,128]{1,0:T(8,128)}, u32[]{:S(2)}) copy-start(f32[1024,128]{1,0:T(8,128)} %param.17) | copy-start | bytes 1572868
  7.2 65.9 %all-gather.26.cloned.1.call-start = ((), (), s32[]{:S(2)}) async-start(), calls=%async_computation.11 | async-start | bytes 1179648 | tf_op jit(solution)/shard_map/all_gather | solution.py:30
  25.8 47.9 %copy-start.10 = (u32[256]{0:T(256)S(1)}, u32[256]{0:T(256)}, u32[]{:S(2)}) copy-start(u32[256]{0:T(256)} %constant.370) | copy-start | bytes 3076
  25.8 59.9 %copy-start.5 = (s32[64,16]{0,1:T(8,128)S(1)}, s32[64,16]{0,1:T(8,128)}, u32[]{:S(2)}) copy-start(s32[64,16]{0,1:T(8,128)} %param.19) | copy-start | bytes 12292
  25.8 59.9 %copy-start.7 = (s32[64]{0:T(128)S(1)}, s32[64]{0:T(128)}, u32[]{:S(2)}) copy-start(s32[64]{0:T(128)} %param.18) | copy-start | bytes 772
  25.8 89.8 %copy-start.9 = (u32[256]{0:T(256)S(1)}, u32[256]{0:T(256)}, u32[]{:S(2)}) copy-start(u32[256]{0:T(256)} %constant.375) | copy-start | bytes 3076
  25.8 90.4 %copy-start.8 = (u32[256]{0:T(256)S(1)}, u32[256]{0:T(256)}, u32[]{:S(2)}) copy-start(u32[256]{0:T(256)} %constant.380) | copy-start | bytes 3076
  25.8 110.9 %copy-start.6 = (f32[1,128]{1,0:T(1,128)S(1)}, f32[1,128]{1,0:T(1,128)}, u32[]{:S(2)}) copy-start(f32[1,128]{1,0:T(1,128)} %param.20) | copy-start | bytes 1540
  25.8 171.2 %all-to-all-start = ((f32[64,1,64,128]{3,2,1,0:T(8,128)}), f32[64,1,64,128]{3,2,1,0:T(8,128)}, u32[]{:S(2)}, u32[]{:S(2)}) async-start(f32[64,1,64,128]{3,2,1,0:T(8,128)} %fusion.48), calls=%async_computation | async-start | bytes 4194304 | tf_op jit(solution)/shard_map/all_to_all | solution.py:113
  40.7 129.5 %all-gather.28.cloned.1.call-start = ((), (), s32[]{:S(2)}) async-start(), calls=%async_computation.12 | async-start | bytes 3145728 | tf_op jit(solution)/shard_map/all_gather | solution.py:30
  292.3 8.4 all-to-all-start.1
  336.4 18.9 %all-to-all-start.3 = ((f32[64,1,1]{2,1,0:T(1,128)}), f32[64,1,1]{2,1,0:T(1,128)S(1)}, u32[]{:S(2)}, u32[]{:S(2)}) async-start(f32[64,1,1]{2,1,0:T(1,128)} %all_to_all.52), calls=%async_computation.3 | async-start | bytes 65536 | tf_op jit(solution)/shard_map/all_to_all | solution.py:83
  355.3 19.7 %all-to-all-start.5 = ((f32[64,1,64]{2,1,0:T(1,128)}), f32[64,1,64]{2,1,0:T(1,128)S(1)}, u32[]{:S(2)}, u32[]{:S(2)}) async-start(f32[64,1,64]{2,1,0:T(1,128)} %copy.297), calls=%async_computation.5 | async-start | bytes 65536 | tf_op jit(solution)/shard_map/all_to_all | solution.py:83
  369.8 13.8 %copy-start.4 = (f32[64,64,64]{0,2,1:T(8,128)S(1)}, f32[64,64,64]{0,2,1:T(8,128)}, u32[]{:S(2)}) copy-start(f32[64,64,64]{0,2,1:T(8,128)} %select_add_fusion.1) | copy-start | bytes 3145732
  375.0 17.9 %all-to-all-start.2 = ((f32[64,1,128]{2,1,0:T(1,128)}), f32[64,1,128]{2,1,0:T(1,128)S(1)}, u32[]{:S(2)}, u32[]{:S(2)}) async-start(f32[64,1,128]{2,1,0:T(1,128)} %bitcast.68), calls=%async_computation.2 | async-start | bytes 65536 | tf_op jit(solution)/shard_map/all_to_all | solution.py:83
  392.9 58.8 %all-to-all-start.4 = ((f32[64,1,64,128]{3,2,1,0:T(8,128)}), f32[64,1,64,128]{3,2,1,0:T(8,128)S(1)}, u32[]{:S(2)}, u32[]{:S(2)}) async-start(f32[64,1,64,128]{3,2,1,0:T(8,128)} %copy.291), calls=%async_computation.4 | async-start | bytes 4194304 | tf_op jit(solution)/shard_map/all_to_all | solution.py:83
  402.0 115.7 %all-gather.30.cloned.1.call-start = ((), (), s32[]{:S(2)}) async-start(), calls=%async_computation.13 | async-start | bytes 1179648 | tf_op jit(solution)/shard_map/all_gather | solution.py:30
  486.2 121.6 %all-gather.32.cloned.1.call-start = ((), (), s32[]{:S(2)}) async-start(), calls=%async_computation.14 | async-start | bytes 3145728 | tf_op jit(solution)/shard_map/all_gather | solution.py:30
  623.0 3.4 copy-start.2
  732.5 8.3 all-to-all-start.6
  777.1 20.9 %all-to-all-start.8 = ((f32[64,1,1]{2,1,0:T(1,128)}), f32[64,1,1]{2,1,0:T(1,128)S(1)}, u32[]{:S(2)}, u32[]{:S(2)}) async-start(f32[64,1,1]{2,1,0:T(1,128)} %all_to_all.53), calls=%async_computation.8 | async-start | bytes 65536 | tf_op jit(solution)/shard_map/all_to_all | solution.py:83
  798.0 19.7 %all-to-all-start.10 = ((f32[64,1,64]{2,1,0:T(1,128)}), f32[64,1,64]{2,1,0:T(1,128)S(1)}, u32[]{:S(2)}, u32[]{:S(2)}) async-start(f32[64,1,64]{2,1,0:T(1,128)} %copy.327), calls=%async_computation.10 | async-start | bytes 65536 | tf_op jit(solution)/shard_map/all_to_all | solution.py:83
  812.5 13.8 %copy-start.3 = (f32[64,64,64]{0,2,1:T(8,128)S(1)}, f32[64,64,64]{0,2,1:T(8,128)}, u32[]{:S(2)}) copy-start(f32[64,64,64]{0,2,1:T(8,128)} %select_add_fusion) | copy-start | bytes 3145732
  817.7 17.9 %all-to-all-start.7 = ((f32[64,1,128]{2,1,0:T(1,128)}), f32[64,1,128]{2,1,0:T(1,128)S(1)}, u32[]{:S(2)}, u32[]{:S(2)}) async-start(f32[64,1,128]{2,1,0:T(1,128)} %bitcast.109), calls=%async_computation.7 | async-start | bytes 65536 | tf_op jit(solution)/shard_map/all_to_all | solution.py:83
  835.7 59.1 %all-to-all-start.9 = ((f32[64,1,64,128]{3,2,1,0:T(8,128)}), f32[64,1,64,128]{3,2,1,0:T(8,128)S(1)}, u32[]{:S(2)}, u32[]{:S(2)}) async-start(f32[64,1,64,128]{3,2,1,0:T(8,128)} %copy.321), calls=%async_computation.9 | async-start | bytes 4194304 | tf_op jit(solution)/shard_map/all_to_all | solution.py:83
  845.1 74.2 %copy-start.1 = (f32[1024,128]{1,0:T(8,128)S(1)}, f32[1024,128]{1,0:T(8,128)}, u32[]{:S(2)}) copy-start(f32[1024,128]{1,0:T(8,128)} %param.17) | copy-start | bytes 1572868
Sparse Core Ops, SparseCore 0:
  20.6 52.4 all-gather.25
  74.9 18.3 all-gather.27
  486.3 31.3 all-gather.29
  519.4 20.0 all-gather.31
where the time goes:
time: 934 us; the launch traced here: 927 us
  local copies, waits for them, and re-layouts  279 us (30%)
  blocking collectives  198 us (21%)
  waiting for transfers between devices  173 us (19%)
  starting transfers between devices  95.3 us (10%)
  other arithmetic  93.8 us (10%)
  matrix products  68 us (7%)
  between operations  19.9 us (2%)
    all_gather x12, blocking collectives, stacked_from(): pieces = lax.all_gather(pieces, axes[k], axis=0, tiled=True)  147 us
    squeeze x32, local copies, waits for them, and re-layouts, densities(): lax.map(block_density, (centres.reshape(members // group_width, group_wid...  135 us
    all_to_all x8, waiting for transfers between devices, summed_on_arrival(): pieces = lax.all_to_all(in_blocks(value, dim, size), axis, 0, 0, tiled=True)  101 us
    all_to_all x8, starting transfers between devices, summed_on_arrival(): pieces = lax.all_to_all(in_blocks(value, dim, size), axis, 0, 0, tiled=True)  71.5 us
    all_gather x4, waiting for transfers between devices, stacked_from(): pieces = lax.all_gather(pieces, axes[k], axis=0, tiled=True)  63.8 us
    unnamed x6, blocking collectives  50.8 us
    unnamed x59, local copies, waits for them, and re-layouts  35.6 us
    dot_general x16, matrix products, block_moments(): jnp.einsum('grd,gre->gde', shifted * weight_block[:, :, None], shifted, p...  33.4 us
  transfers between devices with their start and end apart: 15, of which 10 were waited for; matrix products, arithmetic and copies ran while one was open for 11% of the time, Pallas kernels for 0%

commit v1 on v0

v1 whole, which is shorter than its diff:
```python
import math

import jax
import jax.numpy as jnp
from jax import lax
from jax.experimental import pallas as pl
from jax.experimental.pallas import tpu as pltpu
from jax.sharding import Mesh
from jax.sharding import PartitionSpec as P

D = 128
BR = 64
RB = 4
ITERS = 2
Z, Y, C, X = "dp_0", "dp_1", "dp_2", "comp"
DP = (Z, Y, C)
DP_COMP = (Z, Y, C, X)
NZ, NY, NC, NX = 8, 4, 2, 4
NPTS = NZ * NY * NC * NX * BR
ROWS = NPTS // D
RA, RB_, RC = 24, 24, 16
BASE_B = NZ * NY * NC * NX * RA
BASE_C = BASE_B + NZ * NY * NC * NX * RB_
CHUNK = 1024
LOG_TWO_PI = math.log(2.0 * math.pi)
MESH = pl.DeviceIdType.MESH
F32, BF16 = jnp.float32, jnp.bfloat16
VMEM_LIMIT = 60 * 1024 * 1024


def vmem():
    return pl.BlockSpec(memory_space=pltpu.VMEM)


def smem():
    return pl.BlockSpec(memory_space=pltpu.SMEM)


def here():
    return lax.axis_index(Z), lax.axis_index(Y), lax.axis_index(C), lax.axis_index(X)


def shifted(place, step, size):
    return lax.rem(place + (step + size), size)


def offset_a(k, x, y=0, z=0):
    return (((k * NX + x) * NY + y) * NZ + z) * RA


def offset_b(k, y, z=0, x=0):
    return BASE_B + (((k * NY + y) * NZ + z) * NX + x) * RB_


def offset_c(k, z, x=0, y=0):
    return BASE_C + (((k * NZ + z) * NX + x) * NY + y) * RC


def gather_kernel(
    from_slot, own_slot, slots, out, r1, s2, r2,
    send1, recv1, send2, recv2, sendg, recvg, sends, recvs, sendk, recvk,
):
    z, y, k, x = here()
    side = y * NC + k
    nside = NY * NC

    def side_of(step):
        t = shifted(side, step, nside)
        return {Y: t // NC, C: lax.rem(t, NC)}

    barrier = pltpu.get_barrier_semaphore()
    for step in range(1, nside):
        pl.semaphore_signal(barrier, inc=1, device_id=side_of(step), device_id_type=MESH)
    for step in range(1, NZ):
        pl.semaphore_signal(
            barrier, inc=1, device_id={Z: shifted(z, step, NZ)}, device_id_type=MESH
        )
    for step in range(1, NX):
        pl.semaphore_signal(
            barrier, inc=1, device_id={X: shifted(x, step, NX)}, device_id_type=MESH
        )
    pl.semaphore_wait(barrier, nside - 1 + NZ - 1 + NX - 1)

    def remote(src, dst, ssem, rsem, target):
        return pltpu.make_async_remote_copy(
            src_ref=src, dst_ref=dst, send_sem=ssem, recv_sem=rsem,
            device_id=target, device_id_type=MESH,
        )

    copies = []
    for step in range(1, nside):
        t = shifted(side, step, nside)
        copies.append(
            remote(slots.at[t], r1.at[side], send1.at[step], recv1.at[step], side_of(step))
        )
        copies[-1].start()
    r1[side] = slots[side]
    for copy in copies:
        copy.wait()
    for t in range(NZ):
        s2[t] = r1[from_slot[t]]
    copies = []
    for step in range(1, NZ):
        t = shifted(z, step, NZ)
        copies.append(remote(s2.at[t], r2.at[z], send2.at[step], recv2.at[step], {Z: t}))
        copies[-1].start()
    r2[z] = s2[z]
    for copy in copies:
        copy.wait()
    block = r2[own_slot[0]]

    def rows(start, size):
        return out.at[pl.ds(pl.multiple_of(start, 8), size)]

    rows(offset_a(k, x, y, z), RA)[...] = block[:RA]
    rows(offset_b(k, y, z, x), RB_)[...] = block[RA : RA + RB_]
    rows(offset_c(k, z, x, y), RC)[...] = block[RA + RB_ :]

    number = 0
    stages = (
        (
            (Z, z, NZ, offset_a(k, x, y, z), RA),
            (X, x, NX, offset_b(k, y, z, x), RB_),
            (Y, y, NY, offset_c(k, z, x, y), RC),
        ),
        (
            (Z, z, NZ, offset_b(k, y, z), NX * RB_),
            (Y, y, NY, offset_a(k, x, y), NZ * RA),
            (X, x, NX, offset_c(k, z, x), NY * RC),
        ),
    )
    for stage in stages:
        copies = []
        for axis, place, size, start, count in stage:
            part = rows(start, count)
            for step in range(1, size):
                copies.append(
                    remote(
                        part, part, sendg.at[number], recvg.at[number],
                        {axis: shifted(place, step, size)},
                    )
                )
                copies[-1].start()
                number += 1
        for copy in copies:
            copy.wait()

    other = {C: 1 - k}
    rings = (
        (X, x, NX, lambda at: offset_a(k, at), NY * NZ * RA),
        (Y, y, NY, lambda at: offset_b(k, at), NZ * NX * RB_),
        (Z, z, NZ, lambda at: offset_c(k, at), NX * NY * RC),
    )
    pieces = {}
    waiting = []
    to_other = []
    number = 0

    def pass_on(start, size):
        part = rows(start, size)
        n = len(to_other)
        to_other.append(remote(part, part, sendk.at[n], recvk.at[n], other))
        to_other[-1].start()

    def half_start(start, size, half):
        return start + half * (size // 2)

    def send(ring, way, step, half):
        axis, place, size, start_of, unit = rings[ring]
        start = half_start(start_of(shifted(place, -way * (step - 1), size)), unit, half)
        part = rows(start, unit // 2)
        n = len(waiting)
        copy = remote(
            part, part, sends.at[n], recvs.at[n], {axis: shifted(place, way, size)}
        )
        copy.start()
        waiting.append(copy)
        pieces[ring, way, step, half] = copy

    order = []
    for ring in (0, 1, 2):
        steps = rings[ring][2] // 2
        for step in range(1, steps + 1):
            for late in (0, 1):
                if step == steps and late:
                    continue
                scale = 2.8 if ring < 2 else 1.0
                for way in (1, -1):
                    half = late if way == 1 else 1 - late
                    order.append((scale * (2 * step + late - 1), ring, way, step, half))
    order.sort(key=lambda row: row[0])
    for _, ring, way, step, half in order:
        if step == 1:
            send(ring, way, step, half)
    for axis, place, size, start_of, unit in rings:
        pass_on(start_of(place), unit)
    for _, ring, way, step, half in order:
        axis, place, size, start_of, unit = rings[ring]
        pieces[ring, way, step, half].wait_recv()
        steps = size // 2
        if step + 1 < steps or (step + 1 == steps and half == (0 if way == 1 else 1)):
            send(ring, way, step + 1, half)
        start = half_start(start_of(shifted(place, -way * step, size)), unit, half)
        pass_on(start, unit // 2)
    for copy in waiting:
        copy.wait_send()
    for copy in to_other:
        copy.wait()


N_DIRECT = 2 * (NZ - 1) + 2 * (NX - 1) + 2 * (NY - 1)
N_RING = 2 * (NX - 1) + 2 * (NY - 1) + 2 * (NZ - 1)
N_OTHER = N_RING + 3


def gathered_points(slots, from_slot, own_slot):
    sem = pltpu.SemaphoreType.DMA
    nside = NY * NC
    return pl.pallas_call(
        gather_kernel,
        out_shape=jax.ShapeDtypeStruct((NPTS, D), F32),
        in_specs=[smem(), smem(), vmem()],
        out_specs=vmem(),
        scratch_shapes=[
            pltpu.VMEM((nside, BR, D), F32),
            pltpu.VMEM((NZ, BR, D), F32),
            pltpu.VMEM((NZ, BR, D), F32),
            sem((nside,)), sem((nside,)), sem((NZ,)), sem((NZ,)),
            sem((N_DIRECT,)), sem((N_DIRECT,)),
            sem((N_RING,)), sem((N_RING,)),
            sem((N_OTHER,)), sem((N_OTHER,)),
        ],
        compiler_params=pltpu.CompilerParams(
            collective_id=0, has_side_effects=True, vmem_limit_bytes=VMEM_LIMIT
        ),
        name="gather_points",
    )(from_slot, own_slot, slots)


def live_slots(points, block_counts):
    z, y, k, x = here()
    s = (z * NY + y) * NC + k
    prefix = jnp.cumsum(block_counts) - block_counts
    blocks = points.reshape(-1, BR, D)
    group = NY * NC * NX
    slot = jnp.arange(NY * NC, dtype=jnp.int32) * NX + x
    block = jnp.bitwise_and(slot - prefix[s], group - 1)
    picked = jnp.take(blocks, jnp.minimum(block, blocks.shape[0] - 1), axis=0)
    mine = (y * NC + k) * NX + x
    senders = z * NY * NC + jnp.arange(NY * NC, dtype=jnp.int32)
    j = jnp.bitwise_and(mine - prefix[senders], group - 1)
    live = j < block_counts[senders]
    to_z = (prefix[senders] + j) // group
    targets = jnp.arange(NZ, dtype=jnp.int32)
    hit = ((to_z[None, :] == targets[:, None]) & live[None, :]).astype(jnp.int32)
    from_slot = jnp.sum(hit * jnp.arange(NY * NC, dtype=jnp.int32)[None, :], axis=1)
    own = z * group + mine
    first = jnp.sum((prefix <= own).astype(jnp.int32)) - 1
    own_slot = (first // (NY * NC)).reshape(1)
    return picked, from_slot.astype(jnp.int32), own_slot.astype(jnp.int32)


def lse_kernel(
    table, out, r0, v, rx, u, ry, w, rz,
    send0, recv0, sendx, recvx, sendy, recvy, sendz, recvz, sendo, recvo, sendk, recvk,
):
    z, y, k, x = here()
    other = {C: 1 - k}
    barrier = pltpu.get_barrier_semaphore()
    pl.semaphore_signal(barrier, inc=1, device_id=other, device_id_type=MESH)
    for axis, place, size in ((X, x, NX), (Y, y, NY), (Z, z, NZ)):
        for step in range(1, size):
            pl.semaphore_signal(
                barrier, inc=1, device_id={axis: shifted(place, step, size)},
                device_id_type=MESH,
            )
    pl.semaphore_wait(barrier, 1 + NX - 1 + NY - 1 + NZ - 1)

    def remote(src, dst, ssem, rsem, target):
        return pltpu.make_async_remote_copy(
            src_ref=src, dst_ref=dst, send_sem=ssem, recv_sem=rsem,
            device_id=target, device_id_type=MESH,
        )

    def joined(parts):
        peak = parts[0]
        for part in parts[1:]:
            peak = jnp.maximum(peak, part)
        total = jnp.exp(parts[0] - peak)
        for part in parts[1:]:
            total = total + jnp.exp(part - peak)
        return peak + jnp.log(total)

    copy = remote(table.at[1 - k], r0, send0, recv0, other)
    copy.start()
    copy.wait()
    v[...] = joined([table[k], r0[...]])
    copies = []
    for step in range(1, NX):
        t = shifted(x, step, NX)
        copies.append(
            remote(v.at[t], rx.at[step - 1], sendx.at[step], recvx.at[step], {X: t})
        )
        copies[-1].start()
    for copy in copies:
        copy.wait()
    u[...] = joined([v[x]] + [rx[i] for i in range(NX - 1)])
    copies = []
    for step in range(1, NY):
        copies.append(
            remote(
                u, ry.at[step - 1], sendy.at[step], recvy.at[step], {Y: shifted(y, step, NY)}
            )
        )
        copies[-1].start()
    for copy in copies:
        copy.wait()
    w[...] = joined([u[...]] + [ry[i] for i in range(NY - 1)])
    copies = []
    for step in range(1, NZ):
        copies.append(
            remote(
                w, rz.at[step - 1], sendz.at[step], recvz.at[step], {Z: shifted(z, step, NZ)}
            )
        )
        copies[-1].start()
    for copy in copies:
        copy.wait()
    out[k, x] = joined([w[...]] + [rz[i] for i in range(NZ - 1)])
    copies = []
    for step in range(1, NX):
        part = out.at[k, x]
        copies.append(
            remote(part, part, sendo.at[step], recvo.at[step], {X: shifted(x, step, NX)})
        )
        copies[-1].start()
    to_other = []
    part = out.at[k, x]
    to_other.append(remote(part, part, sendk.at[0], recvk.at[0], other))
    to_other[-1].start()
    for step in range(1, NX):
        copies[step - 1].wait()
        part = out.at[k, shifted(x, -step, NX)]
        to_other.append(remote(part, part, sendk.at[step], recvk.at[step], other))
        to_other[-1].start()
    for copy in to_other:
        copy.wait()


def log_totals(table):
    sem = pltpu.SemaphoreType.DMA
    piece = ROWS // (NC * NX)
    total = pl.pallas_call(
        lse_kernel,
        out_shape=jax.ShapeDtypeStruct((NC, NX, piece, D), F32),
        in_specs=[vmem()],
        out_specs=vmem(),
        scratch_shapes=[
            pltpu.VMEM((NX, piece, D), F32),
            pltpu.VMEM((NX, piece, D), F32),
            pltpu.VMEM((NX - 1, piece, D), F32),
            pltpu.VMEM((piece, D), F32),
            pltpu.VMEM((NY - 1, piece, D), F32),
            pltpu.VMEM((piece, D), F32),
            pltpu.VMEM((NZ - 1, piece, D), F32),
            sem, sem,
            sem((NX,)), sem((NX,)), sem((NY,)), sem((NY,)), sem((NZ,)), sem((NZ,)),
            sem((NX,)), sem((NX,)), sem((NX,)), sem((NX,)),
        ],
        compiler_params=pltpu.CompilerParams(collective_id=1, has_side_effects=True),
        name="log_totals",
    )(table.reshape(NC, NX, piece, D))
    return total.reshape(ROWS, D)


def split2(value):
    high = value.astype(BF16)
    return high, (value - high.astype(F32)).astype(BF16)


def split3(value):
    high = value.astype(BF16)
    rest = value - high.astype(F32)
    middle = rest.astype(BF16)
    return high, middle, (rest - middle.astype(F32)).astype(BF16)


def dot(a, b):
    return jnp.dot(a, b, preferred_element_type=F32)


def eye():
    return (
        lax.broadcasted_iota(jnp.int32, (D, D), 0) == lax.broadcasted_iota(jnp.int32, (D, D), 1)
    ).astype(F32)


def spread(row):
    return jnp.transpose(jnp.broadcast_to(row, (D, D)))


def density(xt_ref, table_ref, mean, factor, weight):
    turned = jnp.transpose(factor)
    high, middle, low = split3(turned)
    main = jnp.concatenate(
        [jnp.concatenate([high, high], axis=1), jnp.concatenate([middle, middle], axis=1)], axis=0
    )
    rest = jnp.concatenate([high, low], axis=1)
    diagonal = jnp.sum(factor * eye(), axis=0, keepdims=True)
    offset = (
        weight + jnp.sum(jnp.log(diagonal), axis=1, keepdims=True) - 0.5 * D * LOG_TWO_PI
    )
    centre = spread(mean)
    groups = CHUNK // D

    def step(i, carry):
        start = pl.multiple_of(i * CHUNK, CHUNK)
        shift = xt_ref[:, pl.ds(start, CHUNK)] - jnp.concatenate([centre] * groups, axis=1)
        a, b, c = split3(shift)
        both = dot(main, jnp.concatenate([a, b], axis=0))
        value = both[:D] + both[D:] + dot(rest, jnp.concatenate([c, a], axis=0))
        row = offset - 0.5 * jnp.sum(value * value, axis=0, keepdims=True)
        for g in range(groups):
            table_ref[pl.ds(i * groups + g, 1), :] = row[:, g * D : (g + 1) * D]
        return carry

    lax.fori_loop(0, NPTS // CHUNK, step, 0)


def turn_points(x_ref, xt_ref):
    def step(i, carry):
        start = pl.multiple_of(i * CHUNK, CHUNK)
        xt_ref[:, pl.ds(start, CHUNK)] = jnp.transpose(x_ref[pl.ds(start, CHUNK), :])
        return carry

    lax.fori_loop(0, NPTS // CHUNK, step, 0)


def first_density_kernel(x_ref, mean_ref, factor_ref, weight_ref, xt_ref, table_ref):
    turn_points(x_ref, xt_ref)
    density(xt_ref, table_ref, mean_ref[...], factor_ref[...], weight_ref[...])


def moments(x_ref, xt_ref, table_ref, total_ref, mean, acc):
    centre = spread(mean)
    groups = CHUNK // D
    acc[...] = jnp.zeros_like(acc)

    def step(i, carry):
        first, count = carry
        start = pl.multiple_of(i * CHUNK, CHUNK)
        at = pl.multiple_of(i * groups, groups)
        share = jnp.exp(table_ref[pl.ds(at, groups), :] - total_ref[pl.ds(at, groups), :])
        wide = jnp.concatenate(
            [jnp.broadcast_to(share[g : g + 1, :], (D, D)) for g in range(groups)], axis=1
        )
        shift = xt_ref[:, pl.ds(start, CHUNK)] - jnp.concatenate([centre] * groups, axis=1)
        scaled = shift * wide
        for g in range(groups):
            first = first + scaled[:, g * D : (g + 1) * D]
        left = jnp.concatenate(split2(scaled), axis=0)
        right = jnp.concatenate(split2(x_ref[pl.ds(start, CHUNK), :] - mean), axis=1)
        acc[...] += dot(left, right)
        return first, count + share

    first, count = lax.fori_loop(
        0, NPTS // CHUNK, step, (jnp.zeros((D, D), F32), jnp.zeros((groups, D), F32))
    )
    weight_sum = jnp.sum(jnp.sum(count, axis=0, keepdims=True), axis=1, keepdims=True)
    first_row = jnp.sum(jnp.transpose(first), axis=0, keepdims=True)
    second = acc[:D, :D] + acc[:D, D:] + acc[D:, :D] + acc[D:, D:]
    return weight_sum, first_row, second


def inverse_factor(covariance, work):
    work[:, :D] = covariance
    work[:, D:] = eye()
    place = lax.broadcasted_iota(jnp.int32, (8, D), 0)
    for p in range(D // 8):
        left = work[8 * p : 8 * p + 8, :D]
        right = work[8 * p : 8 * p + 8, D:]
        columns = [
            jnp.broadcast_to(left[:, 8 * p + a : 8 * p + a + 1], (8, D)) for a in range(8)
        ]
        for a in range(8):
            pivot = jnp.broadcast_to(columns[a][a : a + 1, :], (8, D))
            scale = lax.rsqrt(pivot)
            scale = scale * (1.5 - 0.5 * pivot * scale * scale)
            column = columns[a] * scale
            below = jnp.where(place > a, column, 0.0)
            row_left = jnp.broadcast_to(left[a : a + 1, :], (8, D)) * scale
            row_right = jnp.broadcast_to(right[a : a + 1, :], (8, D)) * scale
            left = jnp.where(place == a, row_left, left - below * row_left)
            right = jnp.where(place == a, row_right, right - below * row_right)
            for b in range(a + 1, 8):
                columns[b] = columns[b] - below * jnp.broadcast_to(column[b : b + 1, :], (8, D))
        work[8 * p : 8 * p + 8, D:] = right
        if p + 1 < D // 8:
            h1, m1, l1 = [part.astype(F32) for part in split3(left)]
            both = jnp.concatenate([left, right], axis=1)
            h2, m2, l2 = [part.astype(F32) for part in split3(both)]
            one = jnp.concatenate([h1, h1, m1, h1, m1, l1], axis=0).astype(BF16)
            two = jnp.concatenate([h2, m2, h2, l2, m2, h2], axis=0).astype(BF16)
            change = lax.dot_general(
                one, two, (((0,), (0,)), ((), ())), preferred_element_type=F32
            )
            work[8 * p + 8 :, :] = work[8 * p + 8 :, :] - change[8 * p + 8 :, :]
    return work[:, D:]


def updated(x_ref, xt_ref, table_ref, total_ref, mean_ref, acc, work):
    mean = mean_ref[...]
    weight_sum, first, second = moments(x_ref, xt_ref, table_ref, total_ref, mean, acc)
    counted = weight_sum + 1.0
    covariance = (second - spread(first) * (first / counted) + eye()) / counted
    covariance = 0.5 * (covariance + jnp.transpose(covariance))
    lower_inverse = inverse_factor(covariance, work)
    new_mean = mean + first / counted
    new_weight = jnp.log(counted / float(NPTS + NZ * NY * NC * NX))
    return new_mean, jnp.transpose(lower_inverse), new_weight


def middle_kernel(
    x_ref, xt_ref, table_ref, total_ref, mean_ref, new_mean_ref, new_table_ref, acc, work
):
    mean, factor, weight = updated(x_ref, xt_ref, table_ref, total_ref, mean_ref, acc, work)
    new_mean_ref[...] = mean
    density(xt_ref, new_table_ref, mean, factor, weight)


def last_kernel(
    x_ref, xt_ref, table_ref, total_ref, mean_ref,
    new_mean_ref, new_factor_ref, new_weight_ref, acc, work,
):
    mean, factor, weight = updated(x_ref, xt_ref, table_ref, total_ref, mean_ref, acc, work)
    new_mean_ref[...] = mean
    new_factor_ref[...] = factor
    new_weight_ref[...] = jnp.broadcast_to(weight, (1, D))


def shape(*dims):
    return jax.ShapeDtypeStruct(dims, F32)


def local_call(kernel, outs, args, scratch, name):
    return pl.pallas_call(
        kernel,
        out_shape=outs,
        in_specs=[vmem()] * len(args),
        out_specs=[vmem()] * len(outs),
        scratch_shapes=scratch,
        compiler_params=pltpu.CompilerParams(vmem_limit_bytes=VMEM_LIMIT),
        name=name,
    )(*args)


SCRATCH = [pltpu.VMEM((2 * D, 2 * D), F32), pltpu.VMEM((D, 2 * D), F32)]


def first_density(x, mean, factor, weight):
    return local_call(
        first_density_kernel, [shape(D, NPTS), shape(ROWS, D)], (x, mean, factor, weight), [],
        "first_density",
    )


def middle(x, xt, table, total, mean):
    return local_call(
        middle_kernel, [shape(1, D), shape(ROWS, D)], (x, xt, table, total, mean), SCRATCH,
        "update_and_density",
    )


def last(x, xt, table, total, mean):
    return local_call(
        last_kernel, [shape(1, D), shape(D, D), shape(1, D)], (x, xt, table, total, mean),
        SCRATCH, "update",
    )


def own_densities(total, block_counts, block_dest):
    d = lax.axis_index(DP)
    prefix = jnp.cumsum(block_counts) - block_counts
    j = jnp.arange(block_dest.shape[1], dtype=jnp.int32)
    mine = ((block_dest == d) & (j[None, :] < block_counts[:, None])).reshape(-1)
    number = (prefix[:, None] + j[None, :]).reshape(-1)
    mine = mine.astype(jnp.int32)
    rank = jnp.cumsum(mine) - mine
    want = jnp.arange(RB, dtype=jnp.int32)
    p = jnp.sum(
        mine[None, :] * (rank[None, :] == want[:, None]).astype(jnp.int32) * number[None, :], axis=1
    )
    x = p % NX
    k = p // NX % NC
    y = p // (NX * NC) % NY
    z = p // (NX * NC * NY)
    flat = total.reshape(-1)
    a = flat[:BASE_B].reshape(-1, RA)[offset_a(k, x, y, z) // RA]
    b = flat[BASE_B:BASE_C].reshape(-1, RB_)[(offset_b(k, y, z, x) - BASE_B) // RB_]
    c = flat[BASE_C:].reshape(-1, RC)[(offset_c(k, z, x, y) - BASE_C) // RC]
    return jnp.concatenate([a, b, c], axis=1).reshape(-1)


def per_device(points, block_counts, block_dest, means, factors, log_weights):
    slots, from_slot, own_slot = live_slots(points, block_counts)
    x = gathered_points(slots, from_slot, own_slot)
    xt, table = first_density(x, means, factors[0], log_weights.reshape(1, 1))
    total = log_totals(table)
    mean, table = middle(x, xt, table, total, means)
    total = log_totals(table)
    new_mean, new_factor, new_weight = last(x, xt, table, total, mean)
    density_out = own_densities(total, block_counts, block_dest) / float(D)
    return new_mean, new_factor[None], new_weight[0, :1], density_out


def solution(mesh):
    split = Mesh(mesh.devices.reshape(NZ, NY, NC, NX), DP_COMP)
    in_specs = (P(DP, None), P(), P(), P(DP_COMP, None), P(DP_COMP, None, None), P(DP_COMP))
    out_specs = (P(DP_COMP, None), P(DP_COMP, None, None), P(DP_COMP), P(DP))
    return jax.shard_map(
        per_device, mesh=split, in_specs=in_specs, out_specs=out_specs, check_vma=False
    )
```

time: 934 us -> 182 us (0.19)
  local copies, waits for them, and re-layouts: 279 us -> 7.15 us
  blocking collectives: 198 us -> 0 us
  waiting for transfers between devices: 173 us -> 0 us
  Pallas kernels: 0 us -> 168 us
  starting transfers between devices: 95.3 us -> 0 us
  other arithmetic: 93.8 us -> 5.02 us
  matrix products: 68 us -> 0 us
  between operations: 19.9 us -> 2.17 us
    pallas_call x0 -> x6, Pallas kernels: none -> 168 us  [the longest x1 63.1 us: gathered_points(): pl.pallas_call(gather_kernel, out_shape=jax.ShapeDtypeStruct((NPTS, D), F...]
    all_gather x12 -> x0, blocking collectives: 147 us -> none  [stacked_from(): pieces = lax.all_gather(pieces, axes[k], axis=0, tiled=True)]
    squeeze x32 -> x0, local copies, waits for them, and re-layouts: 135 us -> none  [densities(): lax.map(block_density, (centres.reshape(members // group_width, group_wid...]
    all_to_all x11 -> x0, waiting for transfers between devices: 109 us -> none  [the longest x8 101 us: summed_on_arrival(): pieces = lax.all_to_all(in_blocks(value, dim, size), axis, 0, 0, tiled=True)]
    all_to_all x11 -> x0, starting transfers between devices: 94.7 us -> none  [the longest x8 71.5 us: summed_on_arrival(): pieces = lax.all_to_all(in_blocks(value, dim, size), axis, 0, 0, tiled=True)]
    dot_general x48 -> x0, matrix products: 67.4 us -> none  [the longest x16 33.4 us: block_moments(): jnp.einsum('grd,gre->gde', shifted * weight_block[:, :, None], shifted, p...]
    all_gather x4 -> x0, waiting for transfers between devices: 63.8 us -> none  [stacked_from(): pieces = lax.all_gather(pieces, axes[k], axis=0, tiled=True)]
    unnamed x6 -> x0, blocking collectives: 50.8 us -> none
  transfers between devices with their start and end apart: 15 -> 0, of which waited for: 10 -> 0; matrix products, arithmetic and copies ran while one was open for 11% -> 0% of each run, Pallas kernels for 0% -> 0%
where the time goes in v1:
time: 182 us
  Pallas kernels  168 us (92%)
  local copies, waits for them, and re-layouts  7.15 us (4%)
  other arithmetic  5.02 us (3%)
  between operations  2.17 us (1%)
    pallas_call x1, Pallas kernels, gathered_points(): pl.pallas_call(gather_kernel, out_shape=jax.ShapeDtypeStruct((NPTS, D), F...  63.1 us
    pallas_call x3, Pallas kernels, local_call(): pl.pallas_call(kernel, out_shape=outs, in_specs=[vmem()] * len(args), out...  60.4 us
    pallas_call x2, Pallas kernels, log_totals(): pl.pallas_call(lse_kernel, out_shape=jax.ShapeDtypeStruct((NC, NX, piece,...  44.4 us

profile of v1, /device:TPU:1, one launch (start us, length us, event | category | flops | bytes accessed | tf_op | source)
XLA Modules:
  0.0 182.2 jit_solution(10049277634079889342)
XLA Ops:
  0.7 0.8 copy.14
  1.5 0.1 reduce-window.20
  1.6 0.1 reduce
  1.7 1.3 fusion.3
  3.0 0.6 gather_fusion
  3.6 1.3 gather_fusion.1
  5.0 0.6 select_reduce_fusion.from_slot
  6.3 0.6 dynamic_slice.3
  6.9 0.7 fusion.7
  7.5 0.6 gather_fusion.2
  8.1 0.7 compare_and_fusion
  8.8 0.8 broadcast_select_fusion.slots
  9.6 63.1 %gather_points.1.x_ref = f32[16384,128]{1,0:T(8,128)} custom-call(s32[8]{0:T(128)} %select_reduce_fusion.from_slot, s32[1]{0:T(128)} %bitcast.2.own_slot, f32[8,64,128]{2,1,0:T(8,128)} %broadcast_select_fusion.slots), custom_call_target="tpu_custom_call" | custom-call | tf_op jit(solution)/shard_map/gather_points/pallas_call | solution.py:219
  73.3 16.4 %first_density.1 = (f32[128,16384]{1,0:T(8,128)}, f32[128,128]{1,0:T(8,128)}) custom-call(f32[16384,128]{1,0:T(8,128)} %gather_points.1.x_ref, f32[1,128]{1,0:T(1,128)} %mean_ref.3, f32[128,128]{1,0:T(8,128)} %bitcast.88, f32[1,1]{1,0:T(1,128)} %bitcast.80.weight_ref), custom_call_target="tpu_custom_call" | custom-call | tf_op jit(solution)/shard_map/first_density/pallas_call | solution.py:546
  89.7 21.8 %log_totals.2 = f32[2,4,16,128]{3,2,1,0:T(8,128)} custom-call(f32[2,4,16,128]{3,2,1,0:T(8,128)} %bitcast.86), custom_call_target="tpu_custom_call" | custom-call | tf_op jit(solution)/shard_map/log_totals/pallas_call | solution.py:353
  111.5 25.3 %update_and_density.1 = (f32[1,128]{1,0:T(1,128)}, f32[128,128]{1,0:T(8,128)}) custom-call(f32[16384,128]{1,0:T(8,128)} %gather_points.1.x_ref, f32[128,16384]{1,0:T(8,128)} %get-tuple-element.11.xt_ref, f32[128,128]{1,0:T(8,128)} %get-tuple-element.12.table_ref, f32[128,128]{1,0:T(8,128)} %bitcast.87, f32[1,128]{1,0:T(1,128)} %mean_ref.3), custom_call_target="tpu_custom_call" | custom-call | tf_op jit(solution)/shard_map/update_and_density/pallas_call | solution.py:546
  136.8 22.6 %log_totals.3 = f32[2,4,16,128]{3,2,1,0:T(8,128)} custom-call(f32[2,4,16,128]{3,2,1,0:T(8,128)} %bitcast.85), custom_call_target="tpu_custom_call" | custom-call | tf_op jit(solution)/shard_map/log_totals/pallas_call | solution.py:353
  159.4 18.7 %update.1 = (f32[1,128]{1,0:T(1,128)}, f32[128,128]{1,0:T(8,128)}, f32[1,128]{1,0:T(1,128)}) custom-call(f32[16384,128]{1,0:T(8,128)} %gather_points.1.x_ref, f32[128,16384]{1,0:T(8,128)} %get-tuple-element.11.xt_ref, f32[128,128]{1,0:T(8,128)} %get-tuple-element.13.table_ref, f32[128,128]{1,0:T(8,128)} %bitcast.83, f32[1,128]{1,0:T(1,128)} %get-tuple-element.14.mean_ref), custom_call_target="tpu_custom_call" | custom-call | tf_op jit(solution)/shard_map/update/pallas_call | solution.py:546
  178.1 0.2 slice.27
  178.4 0.1 add.399
  178.5 0.1 copy.15
  178.6 0.1 reshape.590
  178.8 0.3 reduce-window.21
  179.2 0.1 slice_reduce_fusion
  179.4 0.1 multiply_reduce_fusion
  179.5 0.6 gather_fusion.5
  180.1 0.1 reshape.588
  180.2 0.6 gather_fusion.4
  180.8 0.1 reshape.586
  180.9 0.6 gather_fusion.3
  181.5 0.1 maximum_multiply_fusion
  181.5 0.6 div.113
  (24 shorter events, 0.5 us)
Async XLA Ops:
  0.6 5.6 %copy-start = (f32[1024,128]{1,0:T(8,128)S(1)}, f32[1024,128]{1,0:T(8,128)}, u32[]{:S(2)}) copy-start(f32[1024,128]{1,0:T(8,128)} %param.6) | copy-start | bytes 1572868
  159.4 18.7 %copy-start.2 = (f32[2,4,16,128]{3,2,1,0:T(8,128)S(1)}, f32[2,4,16,128]{3,2,1,0:T(8,128)}, u32[]{:S(2)}) copy-start(f32[2,4,16,128]{3,2,1,0:T(8,128)} %log_totals.3) | copy-start | bytes 196612
  159.4 19.1 %copy-start.1 = (s32[64]{0:T(128)S(1)}, s32[64]{0:T(128)}, u32[]{:S(2)}) copy-start(s32[64]{0:T(128)} %param.7) | copy-start | bytes 772
  159.4 19.1 %copy-start.3 = (s32[64,16]{0,1:T(8,128)S(1)}, s32[64,16]{0,1:T(8,128)}, u32[]{:S(2)}) copy-start(s32[64,16]{0,1:T(8,128)} %param.8) | copy-start | bytes 12292

commit v2 on v0

v2 whole, which is shorter than its diff:
```python
import math

import jax
import jax.numpy as jnp
from jax import lax
from jax.experimental import pallas as pl
from jax.experimental.pallas import tpu as pltpu
from jax.sharding import Mesh
from jax.sharding import PartitionSpec as P

D = 128
BR = 64
RB = 4
ITERS = 2
Z, Y, C, X = "dp_0", "dp_1", "dp_2", "comp"
DP = (Z, Y, C)
DP_COMP = (Z, Y, C, X)
NZ, NY, NC, NX = 8, 4, 2, 4
NPTS = NZ * NY * NC * NX * BR
ROWS = NPTS // D
NB = 16
NSIDE = NY * NC
GROUP = NSIDE * NX
PIECE = ROWS // (NC * NX)
RA, RB_, RC = 24, 24, 16
BASE_B = NZ * NY * NC * NX * RA
BASE_C = BASE_B + NZ * NY * NC * NX * RB_
CHUNK = 2048
LOG_TWO_PI = math.log(2.0 * math.pi)
MESH = pl.DeviceIdType.MESH
F32, BF16 = jnp.float32, jnp.bfloat16
VMEM_LIMIT = 60 * 1024 * 1024


def vmem():
    return pl.BlockSpec(memory_space=pltpu.VMEM)


def smem():
    return pl.BlockSpec(memory_space=pltpu.SMEM)


def here():
    return lax.axis_index(Z), lax.axis_index(Y), lax.axis_index(C), lax.axis_index(X)


def shifted(place, step, size):
    return lax.rem(place + (step + size), size)


def split2(value):
    high = value.astype(BF16)
    return high, (value - high.astype(F32)).astype(BF16)


def split3(value):
    high = value.astype(BF16)
    rest = value - high.astype(F32)
    middle = rest.astype(BF16)
    return high, middle, (rest - middle.astype(F32)).astype(BF16)


def dot(a, b):
    return jnp.dot(a, b, preferred_element_type=F32)


def eye():
    return (
        lax.broadcasted_iota(jnp.int32, (D, D), 0) == lax.broadcasted_iota(jnp.int32, (D, D), 1)
    ).astype(F32)


def spread(row):
    return jnp.transpose(jnp.broadcast_to(row, (D, D)))


def moments(x_ref, xt_ref, table_ref, total_ref, mean, acc):
    centre = spread(mean)
    groups = CHUNK // D
    acc[...] = jnp.zeros_like(acc)

    def step(i, carry):
        first, count = carry
        start = pl.multiple_of(i * CHUNK, CHUNK)
        at = pl.multiple_of(i * groups, groups)
        share = jnp.exp(table_ref[pl.ds(at, groups), :] - total_ref[pl.ds(at, groups), :])
        wide = jnp.concatenate(
            [jnp.broadcast_to(share[g : g + 1, :], (D, D)) for g in range(groups)], axis=1
        )
        shift = xt_ref[:, pl.ds(start, CHUNK)] - jnp.concatenate([centre] * groups, axis=1)
        scaled = shift * wide
        for g in range(groups):
            first = first + scaled[:, g * D : (g + 1) * D]
        left = jnp.concatenate(split2(scaled), axis=0)
        right = jnp.concatenate(split2(x_ref[pl.ds(start, CHUNK), :] - mean), axis=1)
        acc[...] += dot(left, right)
        return first, count + share

    first, count = lax.fori_loop(
        0, NPTS // CHUNK, step, (jnp.zeros((D, D), F32), jnp.zeros((groups, D), F32))
    )
    weight_sum = jnp.sum(jnp.sum(count, axis=0, keepdims=True), axis=1, keepdims=True)
    first_row = jnp.sum(jnp.transpose(first), axis=0, keepdims=True)
    second = acc[:D, :D] + acc[:D, D:] + acc[D:, :D] + acc[D:, D:]
    return weight_sum, first_row, second


def inverse_factor(covariance, work):
    work[:, :D] = covariance
    work[:, D:] = eye()
    place = lax.broadcasted_iota(jnp.int32, (8, D), 0)
    last = D // 8

    def wide(row):
        return jnp.broadcast_to(row, (8, D))

    for p in range(last):
        at = 8 * p
        left, right = work[at : at + 8, :D], work[at : at + 8, D:]
        columns = [wide(left[:, at + a : at + a + 1]) for a in range(8)]
        if p + 1 < last:
            left1, right1 = work[at + 8 : at + 16, :D], work[at + 8 : at + 16, D:]
            columns1 = [wide(left1[:, at + a : at + a + 1]) for a in range(8)]
        for a in range(8):
            pivot = wide(columns[a][a : a + 1, :])
            scale = lax.rsqrt(pivot)
            column = columns[a] * scale
            below = jnp.where(place > a, column, 0.0)
            row_left = wide(left[a : a + 1, :]) * scale
            row_right = wide(right[a : a + 1, :]) * scale
            left = jnp.where(place == a, row_left, left - below * row_left)
            right = jnp.where(place == a, row_right, right - below * row_right)
            across = [wide(column[b : b + 1, :]) for b in range(a + 1, 8)]
            for b in range(a + 1, 8):
                columns[b] = columns[b] - below * across[b - a - 1]
            if p + 1 < last:
                below1 = columns1[a] * scale
                left1 = left1 - below1 * row_left
                right1 = right1 - below1 * row_right
                for b in range(a + 1, 8):
                    columns1[b] = columns1[b] - below1 * across[b - a - 1]
        work[at : at + 8, D:] = right
        if p + 1 < last:
            work[at + 8 : at + 16, :D] = left1
            work[at + 8 : at + 16, D:] = right1
        if p + 2 < last:
            h1, m1, l1 = [part.astype(F32) for part in split3(left)]
            both = jnp.concatenate([left, right], axis=1)
            h2, m2, l2 = [part.astype(F32) for part in split3(both)]
            one = jnp.concatenate([h1, h1, m1, h1, m1, l1], axis=0).astype(BF16)
            two = jnp.concatenate([h2, m2, h2, l2, m2, h2], axis=0).astype(BF16)
            change = lax.dot_general(
                one, two, (((0,), (0,)), ((), ())), preferred_element_type=F32
            )
            work[at + 16 :, :] = work[at + 16 :, :] - change[at + 16 :, :]
    return work[:, D:]


def offset_a(k, x, y=0, z=0):
    return (((k * NX + x) * NY + y) * NZ + z) * RA


def offset_b(k, y, z=0, x=0):
    return BASE_B + (((k * NY + y) * NZ + z) * NX + x) * RB_


def offset_c(k, z, x=0, y=0):
    return BASE_C + (((k * NZ + z) * NX + x) * NY + y) * RC


def remote(src, dst, ssem, rsem, target):
    return pltpu.make_async_remote_copy(
        src_ref=src, dst_ref=dst, send_sem=ssem, recv_sem=rsem,
        device_id=target, device_id_type=MESH,
    )


def side_at(side, step):
    t = shifted(side, step, NSIDE)
    return {Y: t // NC, C: lax.rem(t, NC)}


def enter(z, y, k, x):
    barrier = pltpu.get_barrier_semaphore()
    side = y * NC + k
    targets = [side_at(side, step) for step in range(1, NSIDE)]
    targets += [{Z: shifted(z, step, NZ)} for step in range(1, NZ)]
    targets += [{X: shifted(x, step, NX)} for step in range(1, NX)]
    for target in targets:
        pl.semaphore_signal(barrier, inc=1, device_id=target, device_id_type=MESH)
    return barrier, len(targets)


def choose_blocks(counts, prefix, z, y, k, x):
    mine = (y * NC + k) * NX + x
    own = z * GROUP + mine

    def step(s, carry):
        before, first = carry
        prefix[s] = before
        return before + counts[s], first + (before <= own).astype(jnp.int32)

    _, first = lax.fori_loop(0, NZ * NSIDE, step, (jnp.int32(0), jnp.int32(-1)))
    start = prefix[z * NSIDE + y * NC + k]
    blocks = [
        jnp.minimum(jnp.bitwise_and(t * NX + x - start, GROUP - 1), NB - 1) for t in range(NSIDE)
    ]
    from_slot = [jnp.int32(0)] * NZ
    for t in range(NSIDE):
        sender = z * NSIDE + t
        j = jnp.bitwise_and(mine - prefix[sender], GROUP - 1)
        to_z = jnp.where(j < counts[sender], (prefix[sender] + j) // GROUP, NZ)
        from_slot = [jnp.where(to_z == i, t, from_slot[i]) for i in range(NZ)]
    return blocks, from_slot, first // NSIDE


def log_totals(table, out, r0, v, rx, u, ry, w, rz, sem, z, y, k, x):
    other = {C: 1 - k}
    number = [0]

    def copy_to(src, dst, target):
        n = number[0]
        number[0] += 1
        copy = remote(src, dst, sem.at[0, n], sem.at[1, n], target)
        copy.start()
        return copy

    def joined(parts):
        peak = parts[0]
        for part in parts[1:]:
            peak = jnp.maximum(peak, part)
        total = jnp.exp(parts[0] - peak)
        for part in parts[1:]:
            total = total + jnp.exp(part - peak)
        return peak + jnp.log(total)

    half = ROWS // NC
    copy_to(table.at[pl.ds(pl.multiple_of((1 - k) * half, 8), half)], r0, other).wait()
    v[...] = joined([table[pl.ds(pl.multiple_of(k * half, 8), half), :], r0[...]])

    def piece(at):
        return pl.ds(pl.multiple_of(at * PIECE, 8), PIECE)

    copies = [
        copy_to(v.at[piece(shifted(x, step, NX))], rx.at[step - 1], {X: shifted(x, step, NX)})
        for step in range(1, NX)
    ]
    for copy in copies:
        copy.wait()
    u[...] = joined([v[piece(x), :]] + [rx[i] for i in range(NX - 1)])
    copies = [
        copy_to(u, ry.at[step - 1], {Y: shifted(y, step, NY)}) for step in range(1, NY)
    ]
    for copy in copies:
        copy.wait()
    w[...] = joined([u[...]] + [ry[i] for i in range(NY - 1)])
    copies = [
        copy_to(w, rz.at[step - 1], {Z: shifted(z, step, NZ)}) for step in range(1, NZ)
    ]
    for copy in copies:
        copy.wait()
    mine = piece(k * NX + x)
    out[mine, :] = joined([w[...]] + [rz[i] for i in range(NZ - 1)])
    part = out.at[mine]
    copies = [copy_to(part, part, {X: shifted(x, step, NX)}) for step in range(1, NX)]
    to_other = [copy_to(part, part, other)]
    for step in range(1, NX):
        copies[step - 1].wait()
        part = out.at[piece(k * NX + shifted(x, -step, NX))]
        to_other.append(copy_to(part, part, other))
    for copy in to_other:
        copy.wait()


N_LSE = 1 + 3 * (NX - 1) + 1 + (NY - 1) + (NZ - 1)


def prepare(mean, factor, weight, main, rest, centre, offset):
    high, middle, low = split3(jnp.transpose(factor))
    main[:D, :D] = high
    main[:D, D:] = high
    main[D:, :D] = middle
    main[D:, D:] = middle
    rest[:, :D] = high
    rest[:, D:] = low
    centre[...] = spread(mean)
    diagonal = jnp.sum(factor * eye(), axis=0, keepdims=True)
    offset[...] = jnp.broadcast_to(
        weight + jnp.sum(jnp.log(diagonal), axis=1, keepdims=True) - 0.5 * D * LOG_TWO_PI, (1, D)
    )


def density(turned, table, first_group, main, rest, centre, offset):
    groups = turned.shape[1] // D
    shift = turned - jnp.concatenate([centre[...]] * groups, axis=1)
    a, b, c = split3(shift)
    both = dot(main[...], jnp.concatenate([a, b], axis=0))
    value = both[:D] + both[D:] + dot(rest[...], jnp.concatenate([c, a], axis=0))
    total = jnp.sum(value * value, axis=0, keepdims=True)
    for g in range(groups):
        table[pl.ds(first_group + g, 1), :] = offset[...] - 0.5 * total[:, g * D : (g + 1) * D]


def updated(x_ref, xt_ref, table_ref, total_ref, mean, acc, work):
    weight_sum, first, second = moments(x_ref, xt_ref, table_ref, total_ref, mean, acc)
    counted = weight_sum + 1.0
    covariance = (second - spread(first) * (first / counted) + eye()) / counted
    covariance = 0.5 * (covariance + jnp.transpose(covariance))
    lower_inverse = inverse_factor(covariance, work)
    new_mean = mean + first / counted
    new_weight = jnp.log(counted / float(NPTS + NZ * NY * NC * NX))
    return new_mean, jnp.transpose(lower_inverse), new_weight


def step_kernel(
    counts, points, mean_ref, factor_ref, weight_ref,
    new_mean_ref, new_factor_ref, new_weight_ref, total_ref,
    prefix, slots, r1, s2, r2, out, xt, table1, table2, total1, mean2,
    main, rest, centre, offset, acc, work, sem1, sem2, semg, sems, semk, *joins,
):
    z, y, k, x = here()
    side = y * NC + k
    barrier, arrivals = enter(z, y, k, x)
    blocks, from_slot, own_slot = choose_blocks(counts, prefix, z, y, k, x)
    for t in range(NSIDE):
        slots[t] = points[blocks[t]]
    pl.semaphore_wait(barrier, arrivals)

    copies = []
    for step in range(1, NSIDE):
        copies.append(
            remote(
                slots.at[shifted(side, step, NSIDE)], r1.at[side],
                sem1.at[0, step], sem1.at[1, step], side_at(side, step),
            )
        )
        copies[-1].start()
    r1[side] = slots[side]
    prepare(mean_ref[...], factor_ref[...], weight_ref[...], main, rest, centre, offset)
    for copy in copies:
        copy.wait()
    for t in range(NZ):
        s2[t] = r1[from_slot[t]]
    copies = []
    for step in range(1, NZ):
        t = shifted(z, step, NZ)
        copies.append(remote(s2.at[t], r2.at[z], sem2.at[0, step], sem2.at[1, step], {Z: t}))
        copies[-1].start()
    r2[z] = s2[z]
    for copy in copies:
        copy.wait()
    block = r2[own_slot]

    def rows(start, size):
        return out.at[pl.ds(pl.multiple_of(start, 8), size)]

    rows(offset_a(k, x, y, z), RA)[...] = block[:RA]
    rows(offset_b(k, y, z, x), RB_)[...] = block[RA : RA + RB_]
    rows(offset_c(k, z, x, y), RC)[...] = block[RA + RB_ :]

    number = [0]

    def spread_out(axis, place, size, start, count):
        part = rows(start, count)
        copies = []
        for step in range(1, size):
            n = number[0]
            number[0] += 1
            copies.append(
                remote(
                    part, part, semg.at[0, n], semg.at[1, n], {axis: shifted(place, step, size)}
                )
            )
            copies[-1].start()
        return copies

    def finish(copies):
        for copy in copies:
            copy.wait()

    first_b = spread_out(X, x, NX, offset_b(k, y, z, x), RB_)
    first_c = spread_out(Y, y, NY, offset_c(k, z, x, y), RC)
    first_a = spread_out(Z, z, NZ, offset_a(k, x, y, z), RA)
    finish(first_b)
    second_b = spread_out(Z, z, NZ, offset_b(k, y, z), NX * RB_)
    finish(first_c)
    second_c = spread_out(X, x, NX, offset_c(k, z, x), NY * RC)
    finish(first_a)
    second_a = spread_out(Y, y, NY, offset_a(k, x, y), NZ * RA)

    other = {C: 1 - k}
    rings = (
        (X, x, NX, offset_a, NY * NZ * RA),
        (Y, y, NY, offset_b, NZ * NX * RB_),
        (Z, z, NZ, offset_c, NX * NY * RC),
    )
    pieces = {}
    waiting = []
    to_other = []
    theirs = []

    def start_of(ring, core, at, half):
        return rings[ring][3](core, at) + half * (rings[ring][4] // 2)

    def pass_on(ring, at, half, size):
        part = rows(start_of(ring, k, at, half), size)
        n = len(to_other)
        to_other.append(remote(part, part, semk.at[0, n], semk.at[1, n], other))
        to_other[-1].start()
        theirs.append((start_of(ring, 1 - k, at, half), size))

    def work_out(start, size):
        unit = min(size, 3 * D)
        for i in range(0, size, unit):
            at = pl.multiple_of(start + i, D)
            turned = jnp.transpose(out[pl.ds(at, unit), :])
            xt[:, pl.ds(at, unit)] = turned
            density(turned, table1, at // D, main, rest, centre, offset)

    def send(ring, way, step, half):
        axis, place, size, _, unit = rings[ring]
        at = shifted(place, -way * (step - 1), size)
        part = rows(start_of(ring, k, at, half), unit // 2)
        n = len(waiting)
        copy = remote(
            part, part, sems.at[0, n], sems.at[1, n], {axis: shifted(place, way, size)}
        )
        copy.start()
        waiting.append(copy)
        pieces[ring, way, step, half] = copy

    order = []
    for ring in (0, 1, 2):
        steps = rings[ring][2] // 2
        begin, scale = (16.3, 4.2) if ring < 2 else (11.5, 1.5)
        for step in range(1, steps + 1):
            for late in (0, 1):
                if step == steps and late:
                    continue
                for way in (1, -1):
                    half = late if way == 1 else 1 - late
                    order.append((begin + scale * (2 * step + late - 1), ring, way, step, half))
    order.sort(key=lambda row: row[0])

    def begin_ring(ring):
        for _, other_ring, way, step, half in order:
            if other_ring == ring and step == 1:
                send(ring, way, step, half)
        pass_on(ring, rings[ring][1], 0, rings[ring][4])

    finish(second_c)
    begin_ring(2)
    work_out(start_of(2, k, z, 0), rings[2][4])
    finish(second_a)
    begin_ring(0)
    finish(second_b)
    begin_ring(1)
    work_out(start_of(0, k, x, 0), rings[0][4])
    work_out(start_of(1, k, y, 0), rings[1][4])
    done = 0
    for _, ring, way, step, half in order:
        axis, place, size, _, unit = rings[ring]
        pieces[ring, way, step, half].wait_recv()
        steps = size // 2
        if step + 1 < steps or (step + 1 == steps and half == (0 if way == 1 else 1)):
            send(ring, way, step + 1, half)
        at = shifted(place, -way * step, size)
        pass_on(ring, at, half, unit // 2)
        work_out(start_of(ring, k, at, half), unit // 2)
        to_other[done].wait_recv()
        work_out(*theirs[done])
        done += 1
    while done < len(to_other):
        to_other[done].wait_recv()
        work_out(*theirs[done])
        done += 1
    for copy in waiting + to_other:
        copy.wait_send()

    half = len(joins) // ITERS
    log_totals(table1, total1, *joins[:half], z, y, k, x)
    mean, factor, weight = updated(out, xt, table1, total1, mean_ref[...], acc, work)
    mean2[...] = mean
    prepare(mean, factor, weight, main, rest, centre, offset)

    def again(i, carry):
        start = pl.multiple_of(i * CHUNK, CHUNK)
        density(
            xt[:, pl.ds(start, CHUNK)], table2, i * (CHUNK // D), main, rest, centre, offset
        )
        return carry

    lax.fori_loop(0, NPTS // CHUNK, again, 0)
    log_totals(table2, total_ref, *joins[half:], z, y, k, x)
    mean, factor, weight = updated(out, xt, table2, total_ref, mean2[...], acc, work)
    new_mean_ref[...] = mean
    new_factor_ref[...] = factor
    new_weight_ref[...] = jnp.broadcast_to(weight, (1, D))


N_DIRECT = 2 * (NZ - 1) + 2 * (NX - 1) + 2 * (NY - 1)
N_RING = 2 * (NX - 1) + 2 * (NY - 1) + 2 * (NZ - 1)
N_OTHER = N_RING + 3


def shape(*dims):
    return jax.ShapeDtypeStruct(dims, F32)


def join_scratch():
    return [
        pltpu.VMEM((ROWS // NC, D), F32),
        pltpu.VMEM((ROWS // NC, D), F32),
        pltpu.VMEM((NX - 1, PIECE, D), F32),
        pltpu.VMEM((PIECE, D), F32),
        pltpu.VMEM((NY - 1, PIECE, D), F32),
        pltpu.VMEM((PIECE, D), F32),
        pltpu.VMEM((NZ - 1, PIECE, D), F32),
        pltpu.SemaphoreType.DMA((2, N_LSE)),
    ]


def whole_step(counts, points, mean, factor, weight):
    sem = pltpu.SemaphoreType.DMA
    return pl.pallas_call(
        step_kernel,
        out_shape=[shape(1, D), shape(D, D), shape(1, D), shape(ROWS, D)],
        in_specs=[smem()] + [vmem()] * 4,
        out_specs=[vmem()] * 4,
        scratch_shapes=[
            pltpu.SMEM((NZ * NSIDE,), jnp.int32),
            pltpu.VMEM((NSIDE, BR, D), F32),
            pltpu.VMEM((NSIDE, BR, D), F32),
            pltpu.VMEM((NZ, BR, D), F32),
            pltpu.VMEM((NZ, BR, D), F32),
            pltpu.VMEM((NPTS, D), F32),
            pltpu.VMEM((D, NPTS), F32),
            pltpu.VMEM((ROWS, D), F32),
            pltpu.VMEM((ROWS, D), F32),
            pltpu.VMEM((ROWS, D), F32),
            pltpu.VMEM((1, D), F32),
            pltpu.VMEM((2 * D, 2 * D), BF16),
            pltpu.VMEM((D, 2 * D), BF16),
            pltpu.VMEM((D, D), F32),
            pltpu.VMEM((1, D), F32),
            pltpu.VMEM((2 * D, 2 * D), F32),
            pltpu.VMEM((D, 2 * D), F32),
            sem((2, NSIDE)), sem((2, NZ)), sem((2, N_DIRECT)), sem((2, N_RING)),
            sem((2, N_OTHER)),
        ]
        + join_scratch() * ITERS,
        compiler_params=pltpu.CompilerParams(
            collective_id=0, has_side_effects=True, vmem_limit_bytes=VMEM_LIMIT
        ),
        name="whole_step",
    )(counts, points, mean, factor, weight)


def own_densities(total, block_counts, block_dest):
    d = lax.axis_index(DP)
    prefix = jnp.cumsum(block_counts) - block_counts
    j = jnp.arange(block_dest.shape[1], dtype=jnp.int32)
    mine = ((block_dest == d) & (j[None, :] < block_counts[:, None])).reshape(-1)
    number = (prefix[:, None] + j[None, :]).reshape(-1)
    mine = mine.astype(jnp.int32)
    rank = jnp.cumsum(mine) - mine
    want = jnp.arange(RB, dtype=jnp.int32)
    p = jnp.sum(
        mine[None, :] * (rank[None, :] == want[:, None]).astype(jnp.int32) * number[None, :], axis=1
    )
    x = p % NX
    k = p // NX % NC
    y = p // (NX * NC) % NY
    z = p // (NX * NC * NY)
    flat = total.reshape(-1)
    a = flat[:BASE_B].reshape(-1, RA)[offset_a(k, x, y, z) // RA]
    b = flat[BASE_B:BASE_C].reshape(-1, RB_)[(offset_b(k, y, z, x) - BASE_B) // RB_]
    c = flat[BASE_C:].reshape(-1, RC)[(offset_c(k, z, x, y) - BASE_C) // RC]
    return jnp.concatenate([a, b, c], axis=1).reshape(-1)


def per_device(points, block_counts, block_dest, means, factors, log_weights):
    new_mean, new_factor, new_weight, total = whole_step(
        block_counts, points.reshape(NB, BR, D), means, factors[0], log_weights.reshape(1, 1)
    )
    density_out = own_densities(total, block_counts, block_dest) / float(D)
    return new_mean, new_factor[None], new_weight[0, :1], density_out


def solution(mesh):
    split = Mesh(mesh.devices.reshape(NZ, NY, NC, NX), DP_COMP)
    in_specs = (P(DP, None), P(), P(), P(DP_COMP, None), P(DP_COMP, None, None), P(DP_COMP))
    out_specs = (P(DP_COMP, None), P(DP_COMP, None, None), P(DP_COMP), P(DP))
    return jax.shard_map(
        per_device, mesh=split, in_specs=in_specs, out_specs=out_specs, check_vma=False
    )
```

time: 934 us -> 134 us (0.14)
  local copies, waits for them, and re-layouts: 279 us -> 6.54 us
  blocking collectives: 198 us -> 0 us
  waiting for transfers between devices: 173 us -> 0 us
  Pallas kernels: 0 us -> 124 us
  starting transfers between devices: 95.3 us -> 0 us
  other arithmetic: 93.8 us -> 0.94 us
  matrix products: 68 us -> 0 us
  between operations: 19.9 us -> 2.57 us
    all_gather x12 -> x0, blocking collectives: 147 us -> none  [stacked_from(): pieces = lax.all_gather(pieces, axes[k], axis=0, tiled=True)]
    squeeze x32 -> x0, local copies, waits for them, and re-layouts: 135 us -> none  [densities(): lax.map(block_density, (centres.reshape(members // group_width, group_wid...]
    pallas_call x0 -> x1, Pallas kernels: none -> 124 us  [whole_step(): pl.pallas_call(step_kernel, out_shape=[shape(1, D), shape(D, D), shape(1,...]
    all_to_all x11 -> x0, waiting for transfers between devices: 109 us -> none  [the longest x8 101 us: summed_on_arrival(): pieces = lax.all_to_all(in_blocks(value, dim, size), axis, 0, 0, tiled=True)]
    all_to_all x11 -> x0, starting transfers between devices: 94.7 us -> none  [the longest x8 71.5 us: summed_on_arrival(): pieces = lax.all_to_all(in_blocks(value, dim, size), axis, 0, 0, tiled=True)]
    dot_general x48 -> x0, matrix products: 67.4 us -> none  [the longest x16 33.4 us: block_moments(): jnp.einsum('grd,gre->gde', shifted * weight_block[:, :, None], shifted, p...]
    all_gather x4 -> x0, waiting for transfers between devices: 63.8 us -> none  [stacked_from(): pieces = lax.all_gather(pieces, axes[k], axis=0, tiled=True)]
    unnamed x6 -> x0, blocking collectives: 50.8 us -> none
  transfers between devices with their start and end apart: 15 -> 0, of which waited for: 10 -> 0; matrix products, arithmetic and copies ran while one was open for 11% -> 0% of each run, Pallas kernels for 0% -> 0%
where the time goes in v2:
time: 134 us
  Pallas kernels  124 us (93%)
  local copies, waits for them, and re-layouts  6.54 us (5%)
  between operations  2.57 us (2%)
    pallas_call x1, Pallas kernels, whole_step(): pl.pallas_call(step_kernel, out_shape=[shape(1, D), shape(D, D), shape(1,...  124 us

profile of v2, /device:TPU:1, one launch (start us, length us, event | category | flops | bytes accessed | tf_op | source)
XLA Modules:
  0.0 134.0 jit_solution(15327837382091871876)
XLA Ops:
  0.6 0.0 copy-start.1
  1.3 0.0 copy-start.2
  1.3 0.0 copy-done.1
  1.3 0.6 copy-done.2
  2.0 0.1 copy.14
  2.1 0.1 reshape.504
  2.1 0.1 reshape.503
  2.2 0.3 reduce-window.20
  2.5 0.1 slice.24
  2.6 0.1 slice_reduce_fusion
  2.7 0.1 bitcast_subtract_fusion
  2.8 0.1 copy.16
  2.9 0.1 reduce-window.22
  3.0 0.1 reduce.1
  3.1 0.1 iota_add_fusion
  3.2 0.1 add.295
  3.3 0.1 multiply_reduce_fusion
  3.5 123.9 %whole_step.1 = (f32[1,128]{1,0:T(1,128)}, f32[128,128]{1,0:T(8,128)}, f32[1,128]{1,0:T(1,128)}, f32[128,128]{1,0:T(8,128)}) custom-call(s32[64]{0:T(128)} %counts.1, f32[16,64,128]{2,1,0:T(8,128)} %bitcast.68, f32[1,128]{1,0:T(1,128)} %mean_ref.1, f32[128,128]{1,0:T(8,128)} %bitcast.70, f32[1,1]{1,0:T(1,128)} %bitcast.67.weight_ref), custom_call_target="tpu_custom_call" | custom-call | tf_op jit(solution)/shard_map/whole_step/pallas_call | solution.py:525
  127.4 0.7 slice.27
  128.2 0.8 fusion.8
  128.9 0.1 reshape.497
  129.0 0.6 gather_fusion
  129.6 0.1 reshape.502
  129.7 0.6 gather_fusion.2
  130.2 0.1 reshape.501
  130.4 0.6 gather_fusion.1
  130.9 0.1 maximum_multiply_fusion
  131.0 0.6 div.86
  131.6 0.5 copy.21
  132.2 0.0 copy-done
  132.2 0.6 copy.22
  132.8 0.0 copy-done.3
  (10 shorter events, 0.1 us)
Async XLA Ops:
  0.6 0.7 copy-start.1
  1.3 0.7 copy-start.2
  130.2 1.9 %copy-start = (f32[128,128]{1,0:T(8,128)S(1)}, f32[128,128]{1,0:T(8,128)}, u32[]{:S(2)}) copy-start(f32[128,128]{1,0:T(8,128)} %get-tuple-element.9) | copy-start | bytes 196612
  131.0 0.6 copy-start.4
  132.2 0.7 copy-start.3

commit v3 on v2

--- a/solution.py
+++ b/solution.py
@@ -21,7 +21,8 @@
 NB = 16
 NSIDE = NY * NC
 GROUP = NSIDE * NX
-PIECE = ROWS // (NC * NX)
+PARTS = 2
+PIECE = ROWS // (PARTS * NC * NX)
 RA, RB_, RC = 24, 24, 16
 BASE_B = NZ * NY * NC * NX * RA
 BASE_C = BASE_B + NZ * NY * NC * NX * RB_
@@ -74,16 +75,16 @@
     return jnp.transpose(jnp.broadcast_to(row, (D, D)))
 
 
-def moments(x_ref, xt_ref, table_ref, total_ref, mean, acc):
+def moments(x_ref, xt_ref, table_ref, base, total_ref, mean, acc, part, carry):
     centre = spread(mean)
     groups = CHUNK // D
-    acc[...] = jnp.zeros_like(acc)
+    steps = NPTS // CHUNK // PARTS
 
     def step(i, carry):
         first, count = carry
         start = pl.multiple_of(i * CHUNK, CHUNK)
-        at = pl.multiple_of(i * groups, groups)
-        share = jnp.exp(table_ref[pl.ds(at, groups), :] - total_ref[pl.ds(at, groups), :])
+        at = pl.multiple_of((i - part * steps) * groups, groups)
+        share = jnp.exp(table_ref[pl.ds(base + at, groups), :] - total_ref[pl.ds(at, groups), :])
         wide = jnp.concatenate(
             [jnp.broadcast_to(share[g : g + 1, :], (D, D)) for g in range(groups)], axis=1
         )
@@ -96,9 +97,14 @@
         acc[...] += dot(left, right)
         return first, count + share
 
-    first, count = lax.fori_loop(
-        0, NPTS // CHUNK, step, (jnp.zeros((D, D), F32), jnp.zeros((groups, D), F32))
-    )
+    if part == 0:
+        acc[...] = jnp.zeros_like(acc)
+        carry = (jnp.zeros((D, D), F32), jnp.zeros((groups, D), F32))
+    return lax.fori_loop(part * steps, (part + 1) * steps, step, carry)
+
+
+def moment_sums(acc, carry):
+    first, count = carry
     weight_sum = jnp.sum(jnp.sum(count, axis=0, keepdims=True), axis=1, keepdims=True)
     first_row = jnp.sum(jnp.transpose(first), axis=0, keepdims=True)
     second = acc[:D, :D] + acc[:D, D:] + acc[D:, :D] + acc[D:, D:]
@@ -186,6 +192,7 @@
     targets = [side_at(side, step) for step in range(1, NSIDE)]
     targets += [{Z: shifted(z, step, NZ)} for step in range(1, NZ)]
     targets += [{X: shifted(x, step, NX)} for step in range(1, NX)]
+    targets += [{X: shifted(x, step, NX), C: 1 - k} for step in range(1, NX)]
     for target in targets:
         pl.semaphore_signal(barrier, inc=1, device_id=target, device_id_type=MESH)
     return barrier, len(targets)
@@ -214,8 +221,64 @@
     return blocks, from_slot, first // NSIDE
 
 
-def log_totals(table, out, r0, v, rx, u, ry, w, rz, sem, z, y, k, x):
-    other = {C: 1 - k}
+def own_blocks(dests, counts, prefix, d):
+    def step(s, carry):
+        n, found = carry[0], carry[1:]
+        at = jnp.int32(-1)
+        for j in range(NB):
+            at = jnp.where((dests[j, s] == d) & (j < counts[s]), j, at)
+        number = prefix[s] + at
+        here_too = at >= 0
+        found = [jnp.where(here_too & (n == i), number, found[i]) for i in range(RB)]
+        return (n + here_too.astype(jnp.int32), *found)
+
+    return lax.fori_loop(0, NZ * NSIDE, step, (jnp.int32(0),) * (RB + 1))[1:]
+
+
+def own_density(total, found, density_ref):
+    lane = lax.broadcasted_iota(jnp.int32, (1, D), 1)
+    line = jnp.zeros((1, D), F32)
+    for i in range(RB):
+        p = found[i]
+        x = lax.rem(p, NX)
+        k = lax.rem(lax.div(p, NX), NC)
+        y = lax.rem(lax.div(p, NX * NC), NY)
+        z = lax.div(p, GROUP)
+        parts = (
+            (0, offset_a(k, x, y, z), RA),
+            (RA, offset_b(k, y, z, x), RB_),
+            (RA + RB_, offset_c(k, z, x, y), RC),
+        )
+        for base, start, count in parts:
+            row = lax.div(start, D)
+            first = start - row * D
+            to = (i % 2) * BR + base
+            by = lax.rem(to - first + D, D)
+            one = pltpu.roll(total[pl.ds(row, 1), :], by, 1)
+            two = pltpu.roll(total[pl.ds(jnp.minimum(row + 1, ROWS - 1), 1), :], by, 1)
+            value = jnp.where(lane - to + first < D, one, two)
+            line = jnp.where((lane >= to) & (lane < to + count), value, line)
+        if i % 2:
+            density_ref[i // 2 : i // 2 + 1, :] = line / float(D)
+
+
+def group_at(k, x, step):
+    t = shifted(k * NX + x, step, NC * NX)
+    return t, {C: t // NX, X: lax.rem(t, NX)}
+
+
+def joined(parts):
+    peak = parts[0]
+    for part in parts[1:]:
+        peak = jnp.maximum(peak, part)
+    total = jnp.exp(parts[0] - peak)
+    for part in parts[1:]:
+        total = total + jnp.exp(part - peak)
+    return peak + jnp.log(total)
+
+
+def log_totals(table, base, out, rg, u, ry, w, rz, sem, z, y, k, x):
+    members = NC * NX
     number = [0]
 
     def copy_to(src, dst, target):
@@ -225,54 +288,41 @@
         copy.start()
         return copy
 
-    def joined(parts):
-        peak = parts[0]
-        for part in parts[1:]:
-            peak = jnp.maximum(peak, part)
-        total = jnp.exp(parts[0] - peak)
-        for part in parts[1:]:
-            total = total + jnp.exp(part - peak)
-        return peak + jnp.log(total)
-
-    half = ROWS // NC
-    copy_to(table.at[pl.ds(pl.multiple_of((1 - k) * half, 8), half)], r0, other).wait()
-    v[...] = joined([table[pl.ds(pl.multiple_of(k * half, 8), half), :], r0[...]])
-
-    def piece(at):
-        return pl.ds(pl.multiple_of(at * PIECE, 8), PIECE)
-
-    copies = [
-        copy_to(v.at[piece(shifted(x, step, NX))], rx.at[step - 1], {X: shifted(x, step, NX)})
-        for step in range(1, NX)
-    ]
+    def piece(start, at):
+        return pl.ds(pl.multiple_of(start + at * PIECE, 8), PIECE)
+
+    mine = piece(0, k * NX + x)
+    copies = []
+    for step in range(1, members):
+        at, target = group_at(k, x, step)
+        copies.append(copy_to(table.at[piece(base, at)], rg.at[step - 1], target))
+    yield
     for copy in copies:
         copy.wait()
-    u[...] = joined([v[piece(x), :]] + [rx[i] for i in range(NX - 1)])
+    u[...] = joined([table[piece(base, k * NX + x), :]] + [rg[i] for i in range(members - 1)])
     copies = [
         copy_to(u, ry.at[step - 1], {Y: shifted(y, step, NY)}) for step in range(1, NY)
     ]
+    yield
     for copy in copies:
         copy.wait()
     w[...] = joined([u[...]] + [ry[i] for i in range(NY - 1)])
     copies = [
         copy_to(w, rz.at[step - 1], {Z: shifted(z, step, NZ)}) for step in range(1, NZ)
     ]
+    yield
     for copy in copies:
         copy.wait()
-    mine = piece(k * NX + x)
     out[mine, :] = joined([w[...]] + [rz[i] for i in range(NZ - 1)])
-    part = out.at[mine]
-    copies = [copy_to(part, part, {X: shifted(x, step, NX)}) for step in range(1, NX)]
-    to_other = [copy_to(part, part, other)]
-    for step in range(1, NX):
-        copies[step - 1].wait()
-        part = out.at[piece(k * NX + shifted(x, -step, NX))]
-        to_other.append(copy_to(part, part, other))
-    for copy in to_other:
+    copies = []
+    for step in range(1, members):
+        copies.append(copy_to(out.at[mine], out.at[mine], group_at(k, x, step)[1]))
+    yield
+    for copy in copies:
         copy.wait()
 
 
-N_LSE = 1 + 3 * (NX - 1) + 1 + (NY - 1) + (NZ - 1)
+N_LSE = 2 * (NC * NX - 1) + (NY - 1) + (NZ - 1)
 
 
 def prepare(mean, factor, weight, main, rest, centre, offset):
@@ -301,8 +351,8 @@
         table[pl.ds(first_group + g, 1), :] = offset[...] - 0.5 * total[:, g * D : (g + 1) * D]
 
 
-def updated(x_ref, xt_ref, table_ref, total_ref, mean, acc, work):
-    weight_sum, first, second = moments(x_ref, xt_ref, table_ref, total_ref, mean, acc)
+def updated(mean, acc, carry, work):
+    weight_sum, first, second = moment_sums(acc, carry)
     counted = weight_sum + 1.0
     covariance = (second - spread(first) * (first / counted) + eye()) / counted
     covariance = 0.5 * (covariance + jnp.transpose(covariance))
@@ -313,15 +363,19 @@
 
 
 def step_kernel(
-    counts, points, mean_ref, factor_ref, weight_ref,
-    new_mean_ref, new_factor_ref, new_weight_ref, total_ref,
-    prefix, slots, r1, s2, r2, out, xt, table1, table2, total1, mean2,
-    main, rest, centre, offset, acc, work, sem1, sem2, semg, sems, semk, *joins,
+    counts, dests, points_ref, mean_ref, factor_ref, weight_ref,
+    new_mean_ref, new_factor_ref, new_weight_ref, density_ref,
+    prefix, points, slots, r1, s2, r2, out, xt, table1, table2a, table2b,
+    total1a, total1b, total2a, total2b, total2, mean2,
+    main, rest, centre, offset, acc, work, sem0, sem1, sem2, semg, sems, semk, *joins,
 ):
     z, y, k, x = here()
     side = y * NC + k
+    load = pltpu.make_async_copy(points_ref, points, sem0)
+    load.start()
     barrier, arrivals = enter(z, y, k, x)
     blocks, from_slot, own_slot = choose_blocks(counts, prefix, z, y, k, x)
+    load.wait()
     for t in range(NSIDE):
         slots[t] = points[blocks[t]]
     pl.semaphore_wait(barrier, arrivals)
@@ -347,6 +401,7 @@
         copies.append(remote(s2.at[t], r2.at[z], sem2.at[0, step], sem2.at[1, step], {Z: t}))
         copies[-1].start()
     r2[z] = s2[z]
+    found = own_blocks(dests, counts, prefix, z * NSIDE + side)
     for copy in copies:
         copy.wait()
     block = r2[own_slot]
@@ -477,22 +532,55 @@
     for copy in waiting + to_other:
         copy.wait_send()
 
-    half = len(joins) // ITERS
-    log_totals(table1, total1, *joins[:half], z, y, k, x)
-    mean, factor, weight = updated(out, xt, table1, total1, mean_ref[...], acc, work)
+    each = len(joins) // (ITERS * PARTS)
+
+    sets = [joins[i * each : (i + 1) * each] for i in range(ITERS * PARTS)]
+
+    def finish_totals(flows, tables, sums, mean):
+        for _ in range(3):
+            for flow in flows:
+                next(flow)
+        carry = None
+        for part, flow in enumerate(flows):
+            next(flow, None)
+            table, base = tables[part]
+            carry = moments(out, xt, table, base, sums[part], mean, acc, part, carry)
+        return updated(mean, acc, carry, work)
+
+    def flows_of(tables, sums, own):
+        return [
+            log_totals(*tables[part], sums[part], *own[part], z, y, k, x) for part in range(PARTS)
+        ]
+
+    tables = [(table1, part * (ROWS // PARTS)) for part in range(PARTS)]
+    sums = (total1a, total1b)
+    flows = flows_of(tables, sums, sets[:PARTS])
+    for flow in flows:
+        next(flow)
+    mean, factor, weight = finish_totals(flows, tables, sums, mean_ref[...])
     mean2[...] = mean
     prepare(mean, factor, weight, main, rest, centre, offset)
 
-    def again(i, carry):
-        start = pl.multiple_of(i * CHUNK, CHUNK)
-        density(
-            xt[:, pl.ds(start, CHUNK)], table2, i * (CHUNK // D), main, rest, centre, offset
-        )
-        return carry
-
-    lax.fori_loop(0, NPTS // CHUNK, again, 0)
-    log_totals(table2, total_ref, *joins[half:], z, y, k, x)
-    mean, factor, weight = updated(out, xt, table2, total_ref, mean2[...], acc, work)
+    tables = [(table2a, 0), (table2b, 0)]
+    sums = (total2a, total2b)
+    flows = flows_of(tables, sums, sets[PARTS:])
+    steps = NPTS // CHUNK // PARTS
+    for part, flow in enumerate(flows):
+
+        def again(i, carry):
+            start = pl.multiple_of((part * steps + i) * CHUNK, CHUNK)
+            density(
+                xt[:, pl.ds(start, CHUNK)], tables[part][0], i * (CHUNK // D),
+                main, rest, centre, offset,
+            )
+            return carry
+
+        lax.fori_loop(0, steps, again, 0)
+        next(flow)
+    mean, factor, weight = finish_totals(flows, tables, sums, mean2[...])
+    for part in range(PARTS):
+        total2[part * (ROWS // PARTS) : (part + 1) * (ROWS // PARTS), :] = sums[part][...]
+    own_density(total2, found, density_ref)
     new_mean_ref[...] = mean
     new_factor_ref[...] = factor
     new_weight_ref[...] = jnp.broadcast_to(weight, (1, D))
@@ -509,9 +597,7 @@
 
 def join_scratch():
     return [
-        pltpu.VMEM((ROWS // NC, D), F32),
-        pltpu.VMEM((ROWS // NC, D), F32),
-        pltpu.VMEM((NX - 1, PIECE, D), F32),
+        pltpu.VMEM((NC * NX - 1, PIECE, D), F32),
         pltpu.VMEM((PIECE, D), F32),
         pltpu.VMEM((NY - 1, PIECE, D), F32),
         pltpu.VMEM((PIECE, D), F32),
@@ -520,15 +606,16 @@
     ]
 
 
-def whole_step(counts, points, mean, factor, weight):
+def whole_step(counts, dests, points, mean, factor, weight):
     sem = pltpu.SemaphoreType.DMA
     return pl.pallas_call(
         step_kernel,
-        out_shape=[shape(1, D), shape(D, D), shape(1, D), shape(ROWS, D)],
-        in_specs=[smem()] + [vmem()] * 4,
+        out_shape=[shape(1, D), shape(D, D), shape(1, D), shape(RB * BR // D, D)],
+        in_specs=[smem(), smem(), pl.BlockSpec(memory_space=pl.ANY)] + [vmem()] * 3,
         out_specs=[vmem()] * 4,
         scratch_shapes=[
             pltpu.SMEM((NZ * NSIDE,), jnp.int32),
+            pltpu.VMEM((NB, BR, D), F32),
             pltpu.VMEM((NSIDE, BR, D), F32),
             pltpu.VMEM((NSIDE, BR, D), F32),
             pltpu.VMEM((NZ, BR, D), F32),
@@ -536,7 +623,7 @@
             pltpu.VMEM((NPTS, D), F32),
             pltpu.VMEM((D, NPTS), F32),
             pltpu.VMEM((ROWS, D), F32),
-            pltpu.VMEM((ROWS, D), F32),
+            *[pltpu.VMEM((ROWS // PARTS, D), F32)] * (3 * PARTS),
             pltpu.VMEM((ROWS, D), F32),
             pltpu.VMEM((1, D), F32),
             pltpu.VMEM((2 * D, 2 * D), BF16),
@@ -545,46 +632,23 @@
             pltpu.VMEM((1, D), F32),
             pltpu.VMEM((2 * D, 2 * D), F32),
             pltpu.VMEM((D, 2 * D), F32),
-            sem((2, NSIDE)), sem((2, NZ)), sem((2, N_DIRECT)), sem((2, N_RING)),
+            sem, sem((2, NSIDE)), sem((2, NZ)), sem((2, N_DIRECT)), sem((2, N_RING)),
             sem((2, N_OTHER)),
         ]
-        + join_scratch() * ITERS,
+        + join_scratch() * (ITERS * PARTS),
         compiler_params=pltpu.CompilerParams(
             collective_id=0, has_side_effects=True, vmem_limit_bytes=VMEM_LIMIT
         ),
         name="whole_step",
-    )(counts, points, mean, factor, weight)
-
-
-def own_densities(total, block_counts, block_dest):
-    d = lax.axis_index(DP)
-    prefix = jnp.cumsum(block_counts) - block_counts
-    j = jnp.arange(block_dest.shape[1], dtype=jnp.int32)
-    mine = ((block_dest == d) & (j[None, :] < block_counts[:, None])).reshape(-1)
-    number = (prefix[:, None] + j[None, :]).reshape(-1)
-    mine = mine.astype(jnp.int32)
-    rank = jnp.cumsum(mine) - mine
-    want = jnp.arange(RB, dtype=jnp.int32)
-    p = jnp.sum(
-        mine[None, :] * (rank[None, :] == want[:, None]).astype(jnp.int32) * number[None, :], axis=1
+    )(counts, dests, points, mean, factor, weight)
+
+
+def per_device(points, block_counts, block_dest, means, factors, log_weights):
+    new_mean, new_factor, new_weight, density_out = whole_step(
+        block_counts, block_dest.T, points.reshape(NB, BR, D), means, factors[0],
+        log_weights.reshape(1, 1),
     )
-    x = p % NX
-    k = p // NX % NC
-    y = p // (NX * NC) % NY
-    z = p // (NX * NC * NY)
-    flat = total.reshape(-1)
-    a = flat[:BASE_B].reshape(-1, RA)[offset_a(k, x, y, z) // RA]
-    b = flat[BASE_B:BASE_C].reshape(-1, RB_)[(offset_b(k, y, z, x) - BASE_B) // RB_]
-    c = flat[BASE_C:].reshape(-1, RC)[(offset_c(k, z, x, y) - BASE_C) // RC]
-    return jnp.concatenate([a, b, c], axis=1).reshape(-1)
-
-
-def per_device(points, block_counts, block_dest, means, factors, log_weights):
-    new_mean, new_factor, new_weight, total = whole_step(
-        block_counts, points.reshape(NB, BR, D), means, factors[0], log_weights.reshape(1, 1)
-    )
-    density_out = own_densities(total, block_counts, block_dest) / float(D)
-    return new_mean, new_factor[None], new_weight[0, :1], density_out
+    return new_mean, new_factor[None], new_weight[0, :1], density_out.reshape(-1)
 
 
 def solution(mesh):

time: 134 us -> 124 us (0.925)
  Pallas kernels: 124 us -> 117 us
  local copies, waits for them, and re-layouts: 6.54 us -> 3.83 us
    pallas_call x1, Pallas kernels: 124 us -> 117 us  [whole_step(): pl.pallas_call(step_kernel, out_shape=[shape(1, D), shape(D, D), shape(1,...]
    unnamed x12 -> x9, local copies, waits for them, and re-layouts: 1.84 us -> 3.83 us
    gather x3 -> x0, local copies, waits for them, and re-layouts: 1.68 us -> none  [the longest x1 0.56 us: own_densities(): a = flat[:BASE_B].reshape(-1, RA)[offset_a(k, x, y, z) // RA]]
    slice x3 -> x0, local copies, waits for them, and re-layouts: 1.55 us -> none  [the longest x1 0.76 us: own_densities(): a = flat[:BASE_B].reshape(-1, RA)[offset_a(k, x, y, z) // RA]]
where the time goes in v3:
time: 124 us
  Pallas kernels  117 us (94%)
  local copies, waits for them, and re-layouts  3.83 us (3%)
  between operations  2.47 us (2%)
    pallas_call x1, Pallas kernels, whole_step(): pl.pallas_call(step_kernel, out_shape=[shape(1, D), shape(D, D), shape(1,...  117 us
    unnamed x9, local copies, waits for them, and re-layouts  3.83 us

profile of v3, /device:TPU:1, one launch (start us, length us, event | category | flops | bytes accessed | tf_op | source)
XLA Modules:
  0.0 123.5 jit_solution(12862019592668254547)
XLA Ops:
  1.3 117.2 %whole_step.1 = (f32[1,128]{1,0:T(1,128)}, f32[128,128]{1,0:T(8,128)}, f32[1,128]{1,0:T(1,128)}, f32[2,128]{1,0:T(2,128)}) custom-call(s32[64]{0:T(128)} %counts.1, s32[16,64]{1,0:T(8,128)} %bitcast.12, f32[16,64,128]{2,1,0:T(8,128)} %bitcast.9, f32[1,128]{1,0:T(1,128)} %mean_ref.1, f32[128,128]{1,0:T(8,128)} %bitcast.11, f32[1,1]{1,0:T(1,128)} %bitcast.8.weight_ref), custom_call_target="tpu_custom_call" | custom-call | tf_op jit(solution)/shard_map/whole_step/pallas_call | solution.py:611
  118.5 0.0 copy-start.2
  118.5 0.7 copy-done.2
  119.2 0.5 copy.15
  119.7 0.0 copy-start.1
  119.7 1.5 %copy.16 = f32[1,128,128]{2,1,0:T(8,128)} copy(f32[1,128,128]{2,1,0:T(8,128)} %bitcast.10) | data formatting | bytes 131072
  121.2 0.0 copy-done.1
  121.2 0.0 copy-start
  121.2 0.6 copy-done
  121.8 0.6 copy.18
Async XLA Ops:
  118.5 0.7 copy-start.2
  119.7 1.5 %copy-start.1 = (f32[1,128]{1,0:T(1,128)S(1)}, f32[1,128]{1,0:T(1,128)}, u32[]{:S(2)}) copy-start(f32[1,128]{1,0:T(1,128)} %get-tuple-element.10) | copy-start | bytes 1540
  121.2 0.7 copy-start

commit v4 on v3

--- a/solution.py
+++ b/solution.py
@@ -123,10 +123,12 @@
     for p in range(last):
         at = 8 * p
         left, right = work[at : at + 8, :D], work[at : at + 8, D:]
-        columns = [wide(left[:, at + a : at + a + 1]) for a in range(8)]
+        if p == 0:
+            columns = [wide(left[:, a : a + 1]) for a in range(8)]
         if p + 1 < last:
             left1, right1 = work[at + 8 : at + 16, :D], work[at + 8 : at + 16, D:]
             columns1 = [wide(left1[:, at + a : at + a + 1]) for a in range(8)]
+            following = [wide(left1[:, at + 8 + b : at + 9 + b]) for b in range(8)]
         for a in range(8):
             pivot = wide(columns[a][a : a + 1, :])
             scale = lax.rsqrt(pivot)
@@ -145,10 +147,13 @@
                 right1 = right1 - below1 * row_right
                 for b in range(a + 1, 8):
                     columns1[b] = columns1[b] - below1 * across[b - a - 1]
+                for b in range(8):
+                    following[b] = following[b] - below1 * wide(below1[b : b + 1, :])
         work[at : at + 8, D:] = right
         if p + 1 < last:
             work[at + 8 : at + 16, :D] = left1
             work[at + 8 : at + 16, D:] = right1
+            columns = following
         if p + 2 < last:
             h1, m1, l1 = [part.astype(F32) for part in split3(left)]
             both = jnp.concatenate([left, right], axis=1)
@@ -452,7 +457,6 @@
     pieces = {}
     waiting = []
     to_other = []
-    theirs = []
 
     def start_of(ring, core, at, half):
         return rings[ring][3](core, at) + half * (rings[ring][4] // 2)
@@ -462,7 +466,6 @@
         n = len(to_other)
         to_other.append(remote(part, part, semk.at[0, n], semk.at[1, n], other))
         to_other[-1].start()
-        theirs.append((start_of(ring, 1 - k, at, half), size))
 
     def work_out(start, size):
         unit = min(size, 3 * D)
@@ -512,23 +515,44 @@
     begin_ring(1)
     work_out(start_of(0, k, x, 0), rings[0][4])
     work_out(start_of(1, k, y, 0), rings[1][4])
-    done = 0
-    for _, ring, way, step, half in order:
-        axis, place, size, _, unit = rings[ring]
-        pieces[ring, way, step, half].wait_recv()
-        steps = size // 2
-        if step + 1 < steps or (step + 1 == steps and half == (0 if way == 1 else 1)):
-            send(ring, way, step + 1, half)
-        at = shifted(place, -way * step, size)
-        pass_on(ring, at, half, unit // 2)
-        work_out(start_of(ring, k, at, half), unit // 2)
-        to_other[done].wait_recv()
-        work_out(*theirs[done])
-        done += 1
-    while done < len(to_other):
-        to_other[done].wait_recv()
-        work_out(*theirs[done])
-        done += 1
+    groups = []
+    for event in order:
+        if groups and groups[-1][0][0] == event[0]:
+            groups[-1].append(event)
+        else:
+            groups.append([event])
+
+    def complete(events):
+        units = []
+        for _, ring, way, step, half in events:
+            axis, place, size, _, unit = rings[ring]
+            at = shifted(place, -way * step, size)
+            if ring < 2:
+                units.append((ring, at, half, unit // 2))
+            elif way == 1 if step == size // 2 else half == (1 if way == 1 else 0):
+                units.append((ring, at, 0, unit))
+        return units
+
+    def handle(core, units):
+        for ring, at, half, size in units:
+            work_out(start_of(ring, core, at, half), size)
+
+    copies = list(to_other)
+    units = [(ring, rings[ring][1], 0, rings[ring][4]) for ring in (2, 0, 1)]
+    for events in groups + [[]]:
+        first = len(to_other)
+        for _, ring, way, step, half in events:
+            axis, place, size, _, unit = rings[ring]
+            pieces[ring, way, step, half].wait_recv()
+            steps = size // 2
+            if step + 1 < steps or (step + 1 == steps and half == (0 if way == 1 else 1)):
+                send(ring, way, step + 1, half)
+            pass_on(ring, shifted(place, -way * step, size), half, unit // 2)
+        handle(k, complete(events))
+        for copy in copies:
+            copy.wait_recv()
+        handle(1 - k, units)
+        copies, units = to_other[first:], complete(events)
     for copy in waiting + to_other:
         copy.wait_send()
 

time: 124 us -> 116 us (0.935)
  Pallas kernels: 117 us -> 110 us
    pallas_call x1, Pallas kernels: 117 us -> 110 us  [whole_step(): pl.pallas_call(step_kernel, out_shape=[shape(1, D), shape(D, D), shape(1,...]
where the time goes in v4:
time: 116 us
  Pallas kernels  110 us (95%)
  local copies, waits for them, and re-layouts  3.83 us (3%)
  between operations  2.47 us (2%)
    pallas_call x1, Pallas kernels, whole_step(): pl.pallas_call(step_kernel, out_shape=[shape(1, D), shape(D, D), shape(1,...  110 us
    unnamed x9, local copies, waits for them, and re-layouts  3.83 us

profile of v4, /device:TPU:1, one launch (start us, length us, event | category | flops | bytes accessed | tf_op | source)
XLA Modules:
  0.0 116.1 jit_solution(14960202175781044019)
XLA Ops:
  1.3 109.9 %whole_step.1 = (f32[1,128]{1,0:T(1,128)}, f32[128,128]{1,0:T(8,128)}, f32[1,128]{1,0:T(1,128)}, f32[2,128]{1,0:T(2,128)}) custom-call(s32[64]{0:T(128)} %counts.1, s32[16,64]{1,0:T(8,128)} %bitcast.12, f32[16,64,128]{2,1,0:T(8,128)} %bitcast.9, f32[1,128]{1,0:T(1,128)} %mean_ref.1, f32[128,128]{1,0:T(8,128)} %bitcast.11, f32[1,1]{1,0:T(1,128)} %bitcast.8.weight_ref), custom_call_target="tpu_custom_call" | custom-call | tf_op jit(solution)/shard_map/whole_step/pallas_call | solution.py:635
  111.1 0.0 copy-start.2
  111.1 0.7 copy-done.2
  111.8 0.5 copy.15
  112.3 0.0 copy-start.1
  112.3 1.5 %copy.16 = f32[1,128,128]{2,1,0:T(8,128)} copy(f32[1,128,128]{2,1,0:T(8,128)} %bitcast.10) | data formatting | bytes 131072
  113.8 0.0 copy-done.1
  113.8 0.0 copy-start
  113.8 0.6 copy-done
  114.5 0.6 copy.18
Async XLA Ops:
  111.1 0.7 copy-start.2
  112.3 1.5 %copy-start.1 = (f32[1,128]{1,0:T(1,128)S(1)}, f32[1,128]{1,0:T(1,128)}, u32[]{:S(2)}) copy-start(f32[1,128]{1,0:T(1,128)} %get-tuple-element.10) | copy-start | bytes 1540
  113.8 0.7 copy-start
